TPU v7x, 256 devices: a whole 4x4x8 slice. The times are simulated.
256 devices in a mesh: units: 64 (over x, z, core), expert: 4 (over y).
Axes of the slice: x: 4, y: 4, z: 8, core: 2. Of those that a mesh axis runs over, the one named last changes fastest.
Arguments:
- a_up: float32 [57344, 2048], P(('expert', 'units')), parts along dimension 0, may hold values from -6 to 6
- a_down: float32 [57344, 2048], P(('expert', 'units')), parts along dimension 0, may hold values from -6 to 6
- b_up: float32 [57344, 2048], P(('expert', 'units')), parts along dimension 0, may hold values from -6 to 6
- b_down: float32 [57344, 2048], P(('expert', 'units')), parts along dimension 0, may hold values from -6 to 6
- perm: int32 [57344], P('expert'), parts along dimension 0, may hold values from 0 to 14335, as said below
Outputs:
- merged_up: float32 [57344, 2048], P(('expert', 'units')), parts along dimension 0
- merged_down: float32 [57344, 2048], P(('expert', 'units')), parts along dimension 0
There are 4 independent parts, one for each index of `expert`. A program takes and returns all parts, laid end to end along the dimension named above; each array names one. Nothing has to cross between parts.
Inputs may be any that keep to these rules, and one draw needn't show every extreme that they name: perm names each of the 14336 units once. Cut the units into aligned blocks of 224: of the units of one source block, at most 5 are matched to units of any one destination block, and in every draw some pair of blocks reaches 5. Every source block sends the same list of counts to the destination blocks, in an order that differs from source to source.
All inputs are finite; a program needn't handle non-finite values.
Results may differ from a plain program's by a relative error of at most 0.00002.
Values sent between devices are 32-bit elements; how exact they have to be, the bound alone decides.
No kernel may reach another device: no remote copies, remote signals or barrier semaphores. Data moves between devices by JAX's collectives and lax.ppermute only.
A program may use at most 64 MiB of HBM per device.

v0:
```python
import functools

import jax
import jax.numpy as jnp
from jax import lax
from jax.experimental import pallas as pl
from jax.experimental.pallas import tpu as pltpu
from jax.sharding import Mesh
from jax.sharding import PartitionSpec as P


UNITS = ("units_0", "units_1", "units_2")
EXPERT_UNITS = ("expert", "units_0", "units_1", "units_2")
NX, NZ, NC = 4, 8, 2
COUNT = NX * NZ * NC
LINES = NX * NC
ROWS = 224
LIMIT = 5
WIDTH = 2048
TALL = WIDTH // 128
FLAT = ROWS * TALL
CELL = LIMIT * TALL
BLOCK = LINES * CELL
BIG = 1 << 24
Z_ORDER = (1, 7, 2, 6, 3, 5, 4)
LINE_ORDER = (4, 2, 6, 5, 3, 7, 1)


def unit_at(line, dz, sign):
    x = (lax.axis_index("units_0") + sign * (line >> 1)) & (NX - 1)
    z = (lax.axis_index("units_1") + sign * dz) & (NZ - 1)
    c = (lax.axis_index("units_2") + sign * (line & 1)) & (NC - 1)
    return (x * NZ + z) * NC + c


def offset(row):
    return (row >> 3) * (8 * TALL) + (row & 7)


def extract(keys):
    for r in range(LIMIT):
        low = jnp.min(keys, axis=0, keepdims=True)
        yield r, low
        keys = jnp.where(keys == low, BIG, keys)


def tables_kernel(perm_ref, sends_ref, takes_ref):
    me = lax.axis_index(UNITS)
    perm = perm_ref[...]
    unit = lax.broadcasted_iota(jnp.int32, (ROWS, COUNT), 1)
    row = lax.broadcasted_iota(jnp.int32, (ROWS, COUNT), 0)
    local = perm - me * ROWS
    for r, low in extract(jnp.where((local >= 0) & (local < ROWS), local, BIG)):
        sends_ref[r : r + 1, 0:COUNT] = offset(jnp.where(low >= BIG, 0, low))
    mine = jnp.sum(jnp.where(unit == me, perm, 0), axis=1, keepdims=True)
    local = mine - unit * ROWS
    for r, low in extract(jnp.where((local >= 0) & (local < ROWS), local * 256 + row, BIG)):
        takes_ref[r : r + 1, 0:COUNT] = offset(jnp.where(low >= BIG, ROWS, low & 255))


def row_at(start):
    return pl.ds(start, TALL, stride=8)


def cell(at, r):
    return slice(at * CELL + r * TALL, at * CELL + r * TALL + TALL)


def pack(sends_ref, rows_ref, block, units):
    for at, unit in enumerate(units):
        for r in range(LIMIT):
            block[cell(at, r), :] = rows_ref[row_at(sends_ref[r, unit]), :]


def pack_by_z_kernel(sends_ref, rows_ref, *blocks):
    for dz, block in zip(Z_ORDER + (0,), blocks):
        pack(sends_ref, rows_ref, block, [unit_at(line, dz, 1) for line in range(LINES)])


def pack_by_line_kernel(sends_ref, rows_ref, *blocks):
    for line, block in zip(LINE_ORDER + (0,), blocks):
        pack(sends_ref, rows_ref, block, [unit_at(line, dz, 1) for dz in range(NZ)])


def turn_kernel(*refs):
    sources, targets = refs[:8], refs[-8:]
    for i in range(8):
        for j in range(8):
            targets[j][i * CELL : (i + 1) * CELL, :] = sources[i][j * CELL : (j + 1) * CELL, :]


def merge(takes_ref, own_ref, block, merged, units):
    for at, unit in enumerate(units):
        for r in range(LIMIT):
            start = takes_ref[r, unit]
            own = own_ref[row_at(jnp.where(start < FLAT, start, 0)), :]
            merged[row_at(start), :] = (own + block[cell(at, r), :]) * 0.5


def store(merged, out_ref, sem):
    copy = pltpu.make_async_copy(merged.at[0:FLAT], out_ref, sem)
    copy.start()
    copy.wait()


def unpack_by_line_kernel(takes_ref, own_ref, *refs):
    blocks, (out_ref, merged, sem) = refs[:LINES], refs[LINES:]
    for line, block in enumerate(blocks):
        merge(takes_ref, own_ref, block, merged, [unit_at(line, dz, -1) for dz in range(NZ)])
    store(merged, out_ref, sem)


def unpack_early_kernel(shifts, takes_ref, own_ref, *refs):
    blocks, merged = refs[:-1], refs[-1]
    for dz, block in zip(shifts, blocks):
        merge(takes_ref, own_ref, block, merged, [unit_at(line, dz, -1) for line in range(LINES)])


def unpack_late_kernel(shifts, takes_ref, own_ref, early_ref, *refs):
    blocks, (out_ref, merged, sem) = refs[: len(shifts)], refs[len(shifts) :]
    merged[...] = early_ref[...]
    for dz, block in zip(shifts, blocks):
        merge(takes_ref, own_ref, block, merged, [unit_at(line, dz, -1) for line in range(LINES)])
    store(merged, out_ref, sem)


def tiles_of(x):
    return x.reshape(ROWS // 8, 8, TALL, 128).transpose(0, 2, 1, 3).reshape(FLAT, 128)


def rows_of(x):
    return x.reshape(ROWS // 8, TALL, 8, 128).transpose(0, 2, 1, 3).reshape(ROWS, WIDTH)


def sent(block, dx, dz, dc):
    def at(x, z, c):
        return (x % NX * NZ + z % NZ) * NC + c % NC

    pairs = [
        (at(x, z, c), at(x + dx, z + dz, c + dc)) for x in range(NX) for z in range(NZ) for c in range(NC)
    ]
    return lax.ppermute(block, UNITS, pairs)


def in_order(blocks, order):
    return [blocks[-1]] + [blocks[order.index(i)] for i in range(1, 8)]


def by_z(blocks):
    blocks = list(blocks)
    for dz in Z_ORDER:
        blocks[dz] = sent(blocks[dz], 0, dz, 0)
    return blocks


def by_line(blocks):
    blocks = list(blocks)
    for line in LINE_ORDER:
        blocks[line] = sent(blocks[line], line >> 1, 0, line & 1)
    return blocks


VMEM = pl.BlockSpec(memory_space=pltpu.VMEM)
SMEM = pl.BlockSpec(memory_space=pltpu.SMEM)
HBM = pl.BlockSpec(memory_space=pltpu.HBM)
PACKED = (jax.ShapeDtypeStruct((BLOCK, 128), jnp.float32),) * 8
MERGED = (FLAT + 8 * TALL, 128)
SCRATCH = [pltpu.VMEM(MERGED, jnp.float32), pltpu.SemaphoreType.DMA]


def call(kernel, out, specs, out_specs, scratch=(), flops=500_000_000):
    return pl.pallas_call(
        kernel,
        out_shape=out,
        in_specs=specs,
        out_specs=out_specs,
        scratch_shapes=list(scratch),
        cost_estimate=pl.CostEstimate(flops=flops, bytes_accessed=1 << 20, transcendentals=0),
        compiler_params=pltpu.CompilerParams(vmem_limit_bytes=12 << 20),
    )


def on_device(a_up, a_down, b_up, b_down, perm):
    out = jax.ShapeDtypeStruct((FLAT, 128), jnp.float32)
    table = jax.ShapeDtypeStruct((8, 128), jnp.int32)
    sends, takes = call(tables_kernel, (table, table), [VMEM], (VMEM, VMEM), flops=2_000_000_000)(
        perm.reshape(COUNT, ROWS).T
    )
    down = call(pack_by_z_kernel, PACKED, [SMEM, VMEM], (VMEM,) * 8)(sends, tiles_of(b_down))
    down = by_z(in_order(down, Z_ORDER))
    up = call(pack_by_line_kernel, PACKED, [SMEM, VMEM], (VMEM,) * 8)(sends, tiles_of(b_up))
    up = by_line(in_order(up, LINE_ORDER))
    up = call(turn_kernel, PACKED, [VMEM] * 8, (VMEM,) * 8)(*up)
    up = by_z(up)
    down = call(turn_kernel, PACKED, [VMEM] * 8, (VMEM,) * 8)(*down)
    down = by_line(down)
    merged_down = call(
        unpack_by_line_kernel, out, [SMEM, VMEM] + [VMEM] * LINES, HBM, SCRATCH
    )(takes, tiles_of(a_down), *down)
    late = Z_ORDER[-2:]
    early = (0,) + Z_ORDER[:-2]
    own = tiles_of(a_up)
    merged_up = call(
        functools.partial(unpack_early_kernel, early),
        jax.ShapeDtypeStruct(MERGED, jnp.float32),
        [SMEM, VMEM] + [VMEM] * len(early),
        VMEM,
    )(takes, own, *[up[dz] for dz in early])
    merged_up = call(
        functools.partial(unpack_late_kernel, late), out, [SMEM, VMEM, VMEM] + [VMEM] * len(late), HBM, SCRATCH
    )(takes, own, merged_up, *[up[dz] for dz in late])
    return rows_of(merged_up), rows_of(merged_down)


def solution(mesh):
    finer = Mesh(
        mesh.devices.reshape(NX, NZ, NC, mesh.shape["expert"]),
        ("units_0", "units_1", "units_2", "expert"),
    )
    rows = P(EXPERT_UNITS, None)
    return jax.shard_map(
        on_device,
        mesh=finer,
        in_specs=(rows, rows, rows, rows, P("expert")),
        out_specs=(rows, rows),
        check_vma=False,
    )
```

profile of v0, /device:TPU:8, one launch (start us, length us, event | category | flops | bytes accessed | tf_op | source)
XLA Modules:
  0.0 193.2 jit_solution(24528555878863827)
XLA Ops:
  4.5 2.0 %collective-permute-start.14 = (f32[640,128]{1,0:T(8,128)S(1)}, f32[640,128]{1,0:T(8,128)S(1)}, u32[]{:S(2)}, u32[]{:S(2)}) collective-permute-start(f32[640,128]{1,0:T(8,128)S(1)} %get-tuple-element.55), channel_id=1, source_target_pairs={{0,8},{4,12},{8,16},{12,20},{16,24},{20,28},{24,32},{28,36},{32,40... | collective-permute-start | bytes 983048 | tf_op jit(solution)/shard_map/ppermute | solution.py:142
  6.5 3.3 %collective-permute-start.15 = (f32[640,128]{1,0:T(8,128)S(1)}, f32[640,128]{1,0:T(8,128)S(1)}, u32[]{:S(2)}, u32[]{:S(2)}) collective-permute-start(f32[640,128]{1,0:T(8,128)S(1)} %get-tuple-element.56), channel_id=1, source_target_pairs={{0,16},{4,20},{8,24},{12,28},{16,32},{20,36},{24,40},{28,44},{32,4... | collective-permute-start | bytes 983048 | tf_op jit(solution)/shard_map/ppermute | solution.py:142
  9.7 4.0 %collective-permute-start.16 = (f32[640,128]{1,0:T(8,128)S(1)}, f32[640,128]{1,0:T(8,128)S(1)}, u32[]{:S(2)}, u32[]{:S(2)}) collective-permute-start(f32[640,128]{1,0:T(8,128)S(1)} %get-tuple-element.57), channel_id=1, source_target_pairs={{0,24},{4,28},{8,32},{12,36},{16,40},{20,44},{24,48},{28,52},{32,5... | collective-permute-start | bytes 983048 | tf_op jit(solution)/shard_map/ppermute | solution.py:142
  14.3 4.9 %collective-permute-start.18 = (f32[640,128]{1,0:T(8,128)S(1)}, f32[640,128]{1,0:T(8,128)S(1)}, u32[]{:S(2)}, u32[]{:S(2)}) collective-permute-start(f32[640,128]{1,0:T(8,128)S(1)} %get-tuple-element.59), channel_id=1, source_target_pairs={{0,40},{4,44},{8,48},{12,52},{16,56},{20,60},{24,0},{28,4},{32,8},... | collective-permute-start | bytes 983048 | tf_op jit(solution)/shard_map/ppermute | solution.py:142
  20.6 7.5 %collective-permute-start.19 = (f32[640,128]{1,0:T(8,128)S(1)}, f32[640,128]{1,0:T(8,128)S(1)}, u32[]{:S(2)}, u32[]{:S(2)}) collective-permute-start(f32[640,128]{1,0:T(8,128)S(1)} %get-tuple-element.60), channel_id=1, source_target_pairs={{0,48},{4,52},{8,56},{12,60},{16,0},{20,4},{24,8},{28,12},{32,16},... | collective-permute-start | bytes 983048 | tf_op jit(solution)/shard_map/ppermute | solution.py:142
  28.2 7.9 %collective-permute-done.15.refs_2_ = f32[640,128]{1,0:T(8,128)S(1)} collective-permute-done((f32[640,128]{1,0:T(8,128)S(1)}, f32[640,128]{1,0:T(8,128)S(1)}, u32[]{:S(2)}, u32[]{:S(2)}) %collective-permute-start.15) | collective-permute-done | bytes 327712 | tf_op jit(solution)/shard_map/ppermute | solution.py:142
  36.0 2.3 %collective-permute-start.20 = (f32[640,128]{1,0:T(8,128)S(1)}, f32[640,128]{1,0:T(8,128)S(1)}, u32[]{:S(2)}, u32[]{:S(2)}) collective-permute-start(f32[640,128]{1,0:T(8,128)S(1)} %get-tuple-element.61), channel_id=1, source_target_pairs={{0,56},{4,60},{8,0},{12,4},{16,8},{20,12},{24,16},{28,20},{32,24},... | collective-permute-start | bytes 983048 | tf_op jit(solution)/shard_map/ppermute | solution.py:142
  38.4 22.3 %collective-permute-done.16.refs_3_ = f32[640,128]{1,0:T(8,128)S(1)} collective-permute-done((f32[640,128]{1,0:T(8,128)S(1)}, f32[640,128]{1,0:T(8,128)S(1)}, u32[]{:S(2)}, u32[]{:S(2)}) %collective-permute-start.16) | collective-permute-done | bytes 327712 | tf_op jit(solution)/shard_map/ppermute | solution.py:142
  60.6 1.5 collective-permute-start.1
  63.4 3.8 %collective-permute-done.19.refs_6_ = f32[640,128]{1,0:T(8,128)S(1)} collective-permute-done((f32[640,128]{1,0:T(8,128)S(1)}, f32[640,128]{1,0:T(8,128)S(1)}, u32[]{:S(2)}, u32[]{:S(2)}) %collective-permute-start.19) | collective-permute-done | bytes 327712 | tf_op jit(solution)/shard_map/ppermute | solution.py:142
  67.2 3.0 %collective-permute-start.3 = (f32[640,128]{1,0:T(8,128)S(1)}, f32[640,128]{1,0:T(8,128)S(1)}, u32[]{:S(2)}, u32[]{:S(2)}) collective-permute-start(f32[640,128]{1,0:T(8,128)S(1)} %get-tuple-element.42), channel_id=1, source_target_pairs={{0,128},{4,132},{8,136},{12,140},{16,144},{20,148},{24,152},{28,15... | collective-permute-start | bytes 983048 | tf_op jit(solution)/shard_map/ppermute | solution.py:142
  70.2 1.8 collective-permute-done.20.refs_7_
  72.1 1.6 collective-permute-start.4
  76.2 2.3 %collective-permute-done.2.refs_3_ = f32[640,128]{1,0:T(8,128)S(1)} collective-permute-done((f32[640,128]{1,0:T(8,128)S(1)}, f32[640,128]{1,0:T(8,128)S(1)}, u32[]{:S(2)}, u32[]{:S(2)}) %collective-permute-start.2) | collective-permute-done | bytes 327712 | tf_op jit(solution)/shard_map/ppermute | solution.py:142
  78.8 8.6 %collective-permute-done.3.refs_4_ = f32[640,128]{1,0:T(8,128)S(1)} collective-permute-done((f32[640,128]{1,0:T(8,128)S(1)}, f32[640,128]{1,0:T(8,128)S(1)}, u32[]{:S(2)}, u32[]{:S(2)}) %collective-permute-start.3) | collective-permute-done | bytes 327712 | tf_op jit(solution)/shard_map/ppermute | solution.py:142
  87.4 6.2 %collective-permute-done.4.refs_5_ = f32[640,128]{1,0:T(8,128)S(1)} collective-permute-done((f32[640,128]{1,0:T(8,128)S(1)}, f32[640,128]{1,0:T(8,128)S(1)}, u32[]{:S(2)}, u32[]{:S(2)}) %collective-permute-start.4) | collective-permute-done | bytes 327712 | tf_op jit(solution)/shard_map/ppermute | solution.py:142
  93.6 4.8 %collective-permute-done.6.refs_7_ = f32[640,128]{1,0:T(8,128)S(1)} collective-permute-done((f32[640,128]{1,0:T(8,128)S(1)}, f32[640,128]{1,0:T(8,128)S(1)}, u32[]{:S(2)}, u32[]{:S(2)}) %collective-permute-start.6) | collective-permute-done | bytes 327712 | tf_op jit(solution)/shard_map/ppermute | solution.py:142
  98.6 2.8 %collective-permute-start.7 = (f32[640,128]{1,0:T(8,128)S(1)}, f32[640,128]{1,0:T(8,128)S(1)}, u32[]{:S(2)}, u32[]{:S(2)}) collective-permute-start(f32[640,128]{1,0:T(8,128)S(1)} %get-tuple-element.47), channel_id=1, source_target_pairs={{0,8},{4,12},{8,16},{12,20},{16,24},{20,28},{24,32},{28,36},{32,40... | collective-permute-start | bytes 983048 | tf_op jit(solution)/shard_map/ppermute | solution.py:142
  101.9 5.0 %collective-permute-start.9 = (f32[640,128]{1,0:T(8,128)S(1)}, f32[640,128]{1,0:T(8,128)S(1)}, u32[]{:S(2)}, u32[]{:S(2)}) collective-permute-start(f32[640,128]{1,0:T(8,128)S(1)} %get-tuple-element.49), channel_id=1, source_target_pairs={{0,16},{4,20},{8,24},{12,28},{16,32},{20,36},{24,40},{28,44},{32,4... | collective-permute-start | bytes 983048 | tf_op jit(solution)/shard_map/ppermute | solution.py:142
  107.6 1.8 collective-permute-start.11
  110.3 13.5 %collective-permute-start.12 = (f32[640,128]{1,0:T(8,128)S(1)}, f32[640,128]{1,0:T(8,128)S(1)}, u32[]{:S(2)}, u32[]{:S(2)}) collective-permute-start(f32[640,128]{1,0:T(8,128)S(1)} %get-tuple-element.52), channel_id=1, source_target_pairs={{0,40},{4,44},{8,48},{12,52},{16,56},{20,60},{24,0},{28,4},{32,8},... | collective-permute-start | bytes 983048 | tf_op jit(solution)/shard_map/ppermute | solution.py:142
  123.9 8.0 %collective-permute-done.10.refs_4_ = f32[640,128]{1,0:T(8,128)S(1)} collective-permute-done((f32[640,128]{1,0:T(8,128)S(1)}, f32[640,128]{1,0:T(8,128)S(1)}, u32[]{:S(2)}, u32[]{:S(2)}) %collective-permute-start.10) | collective-permute-done | bytes 327712 | tf_op jit(solution)/shard_map/ppermute | solution.py:142
  131.9 2.7 %collective-permute-start.24 = (f32[640,128]{1,0:T(8,128)S(1)}, f32[640,128]{1,0:T(8,128)S(1)}, u32[]{:S(2)}, u32[]{:S(2)}) collective-permute-start(f32[640,128]{1,0:T(8,128)S(1)} %get-tuple-element.66), channel_id=1, source_target_pairs={{0,128},{4,132},{8,136},{12,140},{16,144},{20,148},{24,152},{28,15... | collective-permute-start | bytes 983048 | tf_op jit(solution)/shard_map/ppermute | solution.py:142
  134.6 30.0 %collective-permute-done.11.refs_5_ = f32[640,128]{1,0:T(8,128)S(1)} collective-permute-done((f32[640,128]{1,0:T(8,128)S(1)}, f32[640,128]{1,0:T(8,128)S(1)}, u32[]{:S(2)}, u32[]{:S(2)}) %collective-permute-start.11) | collective-permute-done | bytes 327712 | tf_op jit(solution)/shard_map/ppermute | solution.py:142
  164.5 2.3 %collective-permute-start.25 = (f32[640,128]{1,0:T(8,128)S(1)}, f32[640,128]{1,0:T(8,128)S(1)}, u32[]{:S(2)}, u32[]{:S(2)}) collective-permute-start(f32[640,128]{1,0:T(8,128)S(1)} %get-tuple-element.67), channel_id=1, source_target_pairs={{0,132},{4,128},{8,140},{12,136},{16,148},{20,144},{24,156},{28,15... | collective-permute-start | bytes 983048 | tf_op jit(solution)/shard_map/ppermute | solution.py:142
  166.8 1.4 collective-permute-start.26
  169.3 1.9 shard_map.71.early_ref
  171.2 2.2 %shard_map.72 = f32[3584,128]{1,0:T(8,128)} custom-call(s32[8,128]{1,0:T(8,128)S(1)} %get-tuple-element.36.takes_ref, f32[3584,128]{1,0:T(8,128)S(1)} %bitcast.32, f32[3712,128]{1,0:T(8,128)S(1)} %shard_map.71.early_ref, f32[640,128]{1,0:T(8,128)S(1)} %collective-permute-done.12.refs_0_, f32[640,128]{1,0:T(8,128)S(1)} %collective-permute-done.13.refs_1_), custom_call_target="tpu_custom_call" | custom-call | flops 500000000 | bytes 1048576 | tf_op jit(solution)/shard_map/pallas_call | solution.py:209
  173.5 2.5 %collective-permute-done.25.refs_5_ = f32[640,128]{1,0:T(8,128)S(1)} collective-permute-done((f32[640,128]{1,0:T(8,128)S(1)}, f32[640,128]{1,0:T(8,128)S(1)}, u32[]{:S(2)}, u32[]{:S(2)}) %collective-permute-start.25) | collective-permute-done | bytes 327712 | tf_op jit(solution)/shard_map/ppermute | solution.py:142
  175.9 6.0 %collective-permute-done.26.refs_6_ = f32[640,128]{1,0:T(8,128)S(1)} collective-permute-done((f32[640,128]{1,0:T(8,128)S(1)}, f32[640,128]{1,0:T(8,128)S(1)}, u32[]{:S(2)}, u32[]{:S(2)}) %collective-permute-start.26) | collective-permute-done | bytes 327712 | tf_op jit(solution)/shard_map/ppermute | solution.py:142
  181.9 7.6 %collective-permute-done.27.refs_7_ = f32[640,128]{1,0:T(8,128)S(1)} collective-permute-done((f32[640,128]{1,0:T(8,128)S(1)}, f32[640,128]{1,0:T(8,128)S(1)}, u32[]{:S(2)}, u32[]{:S(2)}) %collective-permute-start.27) | collective-permute-done | bytes 327712 | tf_op jit(solution)/shard_map/ppermute | solution.py:142
  189.5 3.5 %shard_map.75 = f32[3584,128]{1,0:T(8,128)} custom-call(s32[8,128]{1,0:T(8,128)S(1)} %get-tuple-element.36.takes_ref, f32[3584,128]{1,0:T(8,128)S(1)} %bitcast.33, f32[640,128]{1,0:T(8,128)S(1)} %get-tuple-element.62.refs_0_, f32[640,128]{1,0:T(8,128)S(1)} %collective-permute-done.21.refs_1_, f32[640,128]{1,0:T(8,128)S(1)} %collective-permute-done.22.refs_2_, ...), custom_call_target="tpu_custom_call" | custom-call | flops 500000000 | bytes 1048576 | tf_op jit(solution)/shard_map/pallas_call | solution.py:197
  (42 shorter events, 13.3 us)
Async XLA Ops:
  1.6 1.5 copy-start.2
  2.0 17.2 %copy-start.3 = (f32[224,2048]{1,0:T(8,128)S(1)}, f32[224,2048]{1,0:T(8,128)}, u32[]{:S(2)}) copy-start(f32[224,2048]{1,0:T(8,128)} %param.7) | copy-start | bytes 5505028
  4.5 16.1 %collective-permute-start.14 = (f32[640,128]{1,0:T(8,128)S(1)}, f32[640,128]{1,0:T(8,128)S(1)}, u32[]{:S(2)}, u32[]{:S(2)}) collective-permute-start(f32[640,128]{1,0:T(8,128)S(1)} %get-tuple-element.55), channel_id=1, source_target_pairs={{0,8},{4,12},{8,16},{12,20},{16,24},{20,28},{24,32},{28,36},{32,40... | collective-permute-start | bytes 983048 | tf_op jit(solution)/shard_map/ppermute | solution.py:142
  6.5 29.6 %collective-permute-start.15 = (f32[640,128]{1,0:T(8,128)S(1)}, f32[640,128]{1,0:T(8,128)S(1)}, u32[]{:S(2)}, u32[]{:S(2)}) collective-permute-start(f32[640,128]{1,0:T(8,128)S(1)} %get-tuple-element.56), channel_id=1, source_target_pairs={{0,16},{4,20},{8,24},{12,28},{16,32},{20,36},{24,40},{28,44},{32,4... | collective-permute-start | bytes 983048 | tf_op jit(solution)/shard_map/ppermute | solution.py:142
  9.7 50.9 %collective-permute-start.16 = (f32[640,128]{1,0:T(8,128)S(1)}, f32[640,128]{1,0:T(8,128)S(1)}, u32[]{:S(2)}, u32[]{:S(2)}) collective-permute-start(f32[640,128]{1,0:T(8,128)S(1)} %get-tuple-element.57), channel_id=1, source_target_pairs={{0,24},{4,28},{8,32},{12,36},{16,40},{20,44},{24,48},{28,52},{32,5... | collective-permute-start | bytes 983048 | tf_op jit(solution)/shard_map/ppermute | solution.py:142
  13.8 46.8 %collective-permute-start.17 = (f32[640,128]{1,0:T(8,128)S(1)}, f32[640,128]{1,0:T(8,128)S(1)}, u32[]{:S(2)}, u32[]{:S(2)}) collective-permute-start(f32[640,128]{1,0:T(8,128)S(1)} %get-tuple-element.58), channel_id=1, source_target_pairs={{0,32},{4,36},{8,40},{12,44},{16,48},{20,52},{24,56},{28,60},{32,0... | collective-permute-start | bytes 983048 | tf_op jit(solution)/shard_map/ppermute | solution.py:142
  14.3 47.8 %collective-permute-start.18 = (f32[640,128]{1,0:T(8,128)S(1)}, f32[640,128]{1,0:T(8,128)S(1)}, u32[]{:S(2)}, u32[]{:S(2)}) collective-permute-start(f32[640,128]{1,0:T(8,128)S(1)} %get-tuple-element.59), channel_id=1, source_target_pairs={{0,40},{4,44},{8,48},{12,52},{16,56},{20,60},{24,0},{28,4},{32,8},... | collective-permute-start | bytes 983048 | tf_op jit(solution)/shard_map/ppermute | solution.py:142
  20.6 46.6 %collective-permute-start.19 = (f32[640,128]{1,0:T(8,128)S(1)}, f32[640,128]{1,0:T(8,128)S(1)}, u32[]{:S(2)}, u32[]{:S(2)}) collective-permute-start(f32[640,128]{1,0:T(8,128)S(1)} %get-tuple-element.60), channel_id=1, source_target_pairs={{0,48},{4,52},{8,56},{12,60},{16,0},{20,4},{24,8},{28,12},{32,16},... | collective-permute-start | bytes 983048 | tf_op jit(solution)/shard_map/ppermute | solution.py:142
  36.0 36.0 %collective-permute-start.20 = (f32[640,128]{1,0:T(8,128)S(1)}, f32[640,128]{1,0:T(8,128)S(1)}, u32[]{:S(2)}, u32[]{:S(2)}) collective-permute-start(f32[640,128]{1,0:T(8,128)S(1)} %get-tuple-element.61), channel_id=1, source_target_pairs={{0,56},{4,60},{8,0},{12,4},{16,8},{20,12},{24,16},{28,20},{32,24},... | collective-permute-start | bytes 983048 | tf_op jit(solution)/shard_map/ppermute | solution.py:142
  60.6 13.0 %collective-permute-start = (f32[640,128]{1,0:T(8,128)S(1)}, f32[640,128]{1,0:T(8,128)S(1)}, u32[]{:S(2)}, u32[]{:S(2)}) collective-permute-start(f32[640,128]{1,0:T(8,128)S(1)} %get-tuple-element.39), channel_id=1, source_target_pairs={{0,4},{4,0},{8,12},{12,8},{16,20},{20,16},{24,28},{28,24},{32,36},... | collective-permute-start | bytes 983048 | tf_op jit(solution)/shard_map/ppermute | solution.py:142
  60.6 14.2 %collective-permute-start.1 = (f32[640,128]{1,0:T(8,128)S(1)}, f32[640,128]{1,0:T(8,128)S(1)}, u32[]{:S(2)}, u32[]{:S(2)}) collective-permute-start(f32[640,128]{1,0:T(8,128)S(1)} %get-tuple-element.40), channel_id=1, source_target_pairs={{0,64},{4,68},{8,72},{12,76},{16,80},{20,84},{24,88},{28,92},{32,9... | collective-permute-start | bytes 983048 | tf_op jit(solution)/shard_map/ppermute | solution.py:142
  62.1 16.4 %collective-permute-start.2 = (f32[640,128]{1,0:T(8,128)S(1)}, f32[640,128]{1,0:T(8,128)S(1)}, u32[]{:S(2)}, u32[]{:S(2)}) collective-permute-start(f32[640,128]{1,0:T(8,128)S(1)} %get-tuple-element.41), channel_id=1, source_target_pairs={{0,68},{4,64},{8,76},{12,72},{16,84},{20,80},{24,92},{28,88},{32,1... | collective-permute-start | bytes 983048 | tf_op jit(solution)/shard_map/ppermute | solution.py:142
  67.2 20.2 %collective-permute-start.3 = (f32[640,128]{1,0:T(8,128)S(1)}, f32[640,128]{1,0:T(8,128)S(1)}, u32[]{:S(2)}, u32[]{:S(2)}) collective-permute-start(f32[640,128]{1,0:T(8,128)S(1)} %get-tuple-element.42), channel_id=1, source_target_pairs={{0,128},{4,132},{8,136},{12,140},{16,144},{20,148},{24,152},{28,15... | collective-permute-start | bytes 983048 | tf_op jit(solution)/shard_map/ppermute | solution.py:142
  72.1 21.6 %collective-permute-start.4 = (f32[640,128]{1,0:T(8,128)S(1)}, f32[640,128]{1,0:T(8,128)S(1)}, u32[]{:S(2)}, u32[]{:S(2)}) collective-permute-start(f32[640,128]{1,0:T(8,128)S(1)} %get-tuple-element.43), channel_id=1, source_target_pairs={{0,132},{4,128},{8,140},{12,136},{16,148},{20,144},{24,156},{28,15... | collective-permute-start | bytes 983048 | tf_op jit(solution)/shard_map/ppermute | solution.py:142
  73.6 20.0 %collective-permute-start.5 = (f32[640,128]{1,0:T(8,128)S(1)}, f32[640,128]{1,0:T(8,128)S(1)}, u32[]{:S(2)}, u32[]{:S(2)}) collective-permute-start(f32[640,128]{1,0:T(8,128)S(1)} %get-tuple-element.44), channel_id=1, source_target_pairs={{0,192},{4,196},{8,200},{12,204},{16,208},{20,212},{24,216},{28,22... | collective-permute-start | bytes 983048 | tf_op jit(solution)/shard_map/ppermute | solution.py:142
  74.8 23.6 %collective-permute-start.6 = (f32[640,128]{1,0:T(8,128)S(1)}, f32[640,128]{1,0:T(8,128)S(1)}, u32[]{:S(2)}, u32[]{:S(2)}) collective-permute-start(f32[640,128]{1,0:T(8,128)S(1)} %get-tuple-element.45), channel_id=1, source_target_pairs={{0,196},{4,192},{8,204},{12,200},{16,212},{20,208},{24,220},{28,21... | collective-permute-start | bytes 983048 | tf_op jit(solution)/shard_map/ppermute | solution.py:142
  76.2 93.1 %copy-start = (f32[224,2048]{1,0:T(8,128)S(1)}, f32[224,2048]{1,0:T(8,128)}, u32[]{:S(2)}) copy-start(f32[224,2048]{1,0:T(8,128)} %param.5) | copy-start | bytes 5505028
  78.5 28.4 %collective-permute-start.21 = (f32[640,128]{1,0:T(8,128)S(1)}, f32[640,128]{1,0:T(8,128)S(1)}, u32[]{:S(2)}, u32[]{:S(2)}) collective-permute-start(f32[640,128]{1,0:T(8,128)S(1)} %get-tuple-element.63), channel_id=1, source_target_pairs={{0,4},{4,0},{8,12},{12,8},{16,20},{20,16},{24,28},{28,24},{32,36},... | collective-permute-start | bytes 983048 | tf_op jit(solution)/shard_map/ppermute | solution.py:142
  87.4 20.1 %collective-permute-start.22 = (f32[640,128]{1,0:T(8,128)S(1)}, f32[640,128]{1,0:T(8,128)S(1)}, u32[]{:S(2)}, u32[]{:S(2)}) collective-permute-start(f32[640,128]{1,0:T(8,128)S(1)} %get-tuple-element.64), channel_id=1, source_target_pairs={{0,64},{4,68},{8,72},{12,76},{16,80},{20,84},{24,88},{28,92},{32,9... | collective-permute-start | bytes 983048 | tf_op jit(solution)/shard_map/ppermute | solution.py:142
  98.6 11.7 %collective-permute-start.7 = (f32[640,128]{1,0:T(8,128)S(1)}, f32[640,128]{1,0:T(8,128)S(1)}, u32[]{:S(2)}, u32[]{:S(2)}) collective-permute-start(f32[640,128]{1,0:T(8,128)S(1)} %get-tuple-element.47), channel_id=1, source_target_pairs={{0,8},{4,12},{8,16},{12,20},{16,24},{20,28},{24,32},{28,36},{32,40... | collective-permute-start | bytes 983048 | tf_op jit(solution)/shard_map/ppermute | solution.py:142
  101.4 22.4 %collective-permute-start.8 = (f32[640,128]{1,0:T(8,128)S(1)}, f32[640,128]{1,0:T(8,128)S(1)}, u32[]{:S(2)}, u32[]{:S(2)}) collective-permute-start(f32[640,128]{1,0:T(8,128)S(1)} %get-tuple-element.48), channel_id=1, source_target_pairs={{0,56},{4,60},{8,0},{12,4},{16,8},{20,12},{24,16},{28,20},{32,24},... | collective-permute-start | bytes 983048 | tf_op jit(solution)/shard_map/ppermute | solution.py:142
  101.9 21.9 %collective-permute-start.9 = (f32[640,128]{1,0:T(8,128)S(1)}, f32[640,128]{1,0:T(8,128)S(1)}, u32[]{:S(2)}, u32[]{:S(2)}) collective-permute-start(f32[640,128]{1,0:T(8,128)S(1)} %get-tuple-element.49), channel_id=1, source_target_pairs={{0,16},{4,20},{8,24},{12,28},{16,32},{20,36},{24,40},{28,44},{32,4... | collective-permute-start | bytes 983048 | tf_op jit(solution)/shard_map/ppermute | solution.py:142
  107.0 24.9 %collective-permute-start.10 = (f32[640,128]{1,0:T(8,128)S(1)}, f32[640,128]{1,0:T(8,128)S(1)}, u32[]{:S(2)}, u32[]{:S(2)}) collective-permute-start(f32[640,128]{1,0:T(8,128)S(1)} %get-tuple-element.50), channel_id=1, source_target_pairs={{0,48},{4,52},{8,56},{12,60},{16,0},{20,4},{24,8},{28,12},{32,16},... | collective-permute-start | bytes 983048 | tf_op jit(solution)/shard_map/ppermute | solution.py:142
  107.6 57.0 %collective-permute-start.11 = (f32[640,128]{1,0:T(8,128)S(1)}, f32[640,128]{1,0:T(8,128)S(1)}, u32[]{:S(2)}, u32[]{:S(2)}) collective-permute-start(f32[640,128]{1,0:T(8,128)S(1)} %get-tuple-element.51), channel_id=1, source_target_pairs={{0,24},{4,28},{8,32},{12,36},{16,40},{20,44},{24,48},{28,52},{32,5... | collective-permute-start | bytes 983048 | tf_op jit(solution)/shard_map/ppermute | solution.py:142
  110.3 56.6 %collective-permute-start.12 = (f32[640,128]{1,0:T(8,128)S(1)}, f32[640,128]{1,0:T(8,128)S(1)}, u32[]{:S(2)}, u32[]{:S(2)}) collective-permute-start(f32[640,128]{1,0:T(8,128)S(1)} %get-tuple-element.52), channel_id=1, source_target_pairs={{0,40},{4,44},{8,48},{12,52},{16,56},{20,60},{24,0},{28,4},{32,8},... | collective-permute-start | bytes 983048 | tf_op jit(solution)/shard_map/ppermute | solution.py:142
  123.8 44.4 %collective-permute-start.13 = (f32[640,128]{1,0:T(8,128)S(1)}, f32[640,128]{1,0:T(8,128)S(1)}, u32[]{:S(2)}, u32[]{:S(2)}) collective-permute-start(f32[640,128]{1,0:T(8,128)S(1)} %get-tuple-element.53), channel_id=1, source_target_pairs={{0,32},{4,36},{8,40},{12,44},{16,48},{20,52},{24,56},{28,60},{32,0... | collective-permute-start | bytes 983048 | tf_op jit(solution)/shard_map/ppermute | solution.py:142
  123.8 49.6 %collective-permute-start.23 = (f32[640,128]{1,0:T(8,128)S(1)}, f32[640,128]{1,0:T(8,128)S(1)}, u32[]{:S(2)}, u32[]{:S(2)}) collective-permute-start(f32[640,128]{1,0:T(8,128)S(1)} %get-tuple-element.65), channel_id=1, source_target_pairs={{0,68},{4,64},{8,76},{12,72},{16,84},{20,80},{24,92},{28,88},{32,1... | collective-permute-start | bytes 983048 | tf_op jit(solution)/shard_map/ppermute | solution.py:142
  131.9 41.6 %collective-permute-start.24 = (f32[640,128]{1,0:T(8,128)S(1)}, f32[640,128]{1,0:T(8,128)S(1)}, u32[]{:S(2)}, u32[]{:S(2)}) collective-permute-start(f32[640,128]{1,0:T(8,128)S(1)} %get-tuple-element.66), channel_id=1, source_target_pairs={{0,128},{4,132},{8,136},{12,140},{16,144},{20,148},{24,152},{28,15... | collective-permute-start | bytes 983048 | tf_op jit(solution)/shard_map/ppermute | solution.py:142
  164.5 11.4 %collective-permute-start.25 = (f32[640,128]{1,0:T(8,128)S(1)}, f32[640,128]{1,0:T(8,128)S(1)}, u32[]{:S(2)}, u32[]{:S(2)}) collective-permute-start(f32[640,128]{1,0:T(8,128)S(1)} %get-tuple-element.67), channel_id=1, source_target_pairs={{0,132},{4,128},{8,140},{12,136},{16,148},{20,144},{24,156},{28,15... | collective-permute-start | bytes 983048 | tf_op jit(solution)/shard_map/ppermute | solution.py:142
  166.8 15.1 %collective-permute-start.26 = (f32[640,128]{1,0:T(8,128)S(1)}, f32[640,128]{1,0:T(8,128)S(1)}, u32[]{:S(2)}, u32[]{:S(2)}) collective-permute-start(f32[640,128]{1,0:T(8,128)S(1)} %get-tuple-element.68), channel_id=1, source_target_pairs={{0,192},{4,196},{8,200},{12,204},{16,208},{20,212},{24,216},{28,22... | collective-permute-start | bytes 983048 | tf_op jit(solution)/shard_map/ppermute | solution.py:142
  168.2 21.3 %collective-permute-start.27 = (f32[640,128]{1,0:T(8,128)S(1)}, f32[640,128]{1,0:T(8,128)S(1)}, u32[]{:S(2)}, u32[]{:S(2)}) collective-permute-start(f32[640,128]{1,0:T(8,128)S(1)} %get-tuple-element.69), channel_id=1, source_target_pairs={{0,196},{4,192},{8,204},{12,200},{16,212},{20,208},{24,220},{28,21... | collective-permute-start | bytes 983048 | tf_op jit(solution)/shard_map/ppermute | solution.py:142
  171.2 18.3 %copy-start.1 = (f32[224,2048]{1,0:T(8,128)S(1)}, f32[224,2048]{1,0:T(8,128)}, u32[]{:S(2)}) copy-start(f32[224,2048]{1,0:T(8,128)} %param.6) | copy-start | bytes 5505028
where the time goes:
time: 194 us; the launch traced here: 193 us
  waiting for transfers between devices  113 us (58%)
  starting transfers between devices  66.6 us (34%)
  Pallas kernels  11 us (6%)
  local copies, waits for them, and re-layouts  2.12 us (1%)
    ppermute x28, waiting for transfers between devices, sent(): return lax.ppermute(block, UNITS, pairs)  113 us
    ppermute x28, starting transfers between devices, sent(): return lax.ppermute(block, UNITS, pairs)  66.6 us
  transfers between devices with their start and end apart: 28, of which 14 were waited for; matrix products, arithmetic and copies ran while one was open for 0% of the time, Pallas kernels for 3%

commit v1 on v0

--- a/solution.py
+++ b/solution.py
@@ -22,7 +22,8 @@
 CELL = LIMIT * TALL
 BLOCK = LINES * CELL
 BIG = 1 << 24
-Z_ORDER = (1, 7, 2, 6, 3, 5, 4)
+Z_ORDER = (4, 3, 5, 2, 6, 1, 7)
+Z_LAST = (1, 7, 2, 6, 3, 5, 4)
 LINE_ORDER = (4, 2, 6, 5, 3, 7, 1)
 
 
@@ -44,15 +45,35 @@
         keys = jnp.where(keys == low, BIG, keys)
 
 
+def by_target(perm):
+    lines = COUNT * ROWS // 128
+    line = lax.broadcasted_iota(jnp.int32, (lines, COUNT), 0)
+    first = (lax.broadcasted_iota(jnp.int32, (lines, COUNT), 1) * ROWS) >> 7
+    high = (perm >> 7).astype(jnp.float32)
+    low = (perm & 127).astype(jnp.float32)
+    parts = []
+    for k in range(3):
+        pick = jnp.where(line == first + k, 1.0, 0.0)
+        high_k, low_k = (
+            lax.dot_general(x, pick, (((0,), (0,)), ((), ())), preferred_element_type=jnp.float32)
+            for x in (high, low)
+        )
+        parts.append(high_k.astype(jnp.int32) * 128 + low_k.astype(jnp.int32))
+    whole = jnp.concatenate(parts, axis=0)
+    skip = (lax.broadcasted_iota(jnp.int32, whole.shape, 1) * ROWS) & 127
+    row = lax.broadcasted_iota(jnp.int32, whole.shape, 0) - skip
+    return jnp.where((row >= 0) & (row < ROWS), whole, -1), row
+
+
 def tables_kernel(perm_ref, sends_ref, takes_ref):
     me = lax.axis_index(UNITS)
-    perm = perm_ref[...]
-    unit = lax.broadcasted_iota(jnp.int32, (ROWS, COUNT), 1)
-    row = lax.broadcasted_iota(jnp.int32, (ROWS, COUNT), 0)
+    perm, row = by_target(perm_ref[...])
+    unit = lax.broadcasted_iota(jnp.int32, perm.shape, 1)
     local = perm - me * ROWS
     for r, low in extract(jnp.where((local >= 0) & (local < ROWS), local, BIG)):
         sends_ref[r : r + 1, 0:COUNT] = offset(jnp.where(low >= BIG, 0, low))
     mine = jnp.sum(jnp.where(unit == me, perm, 0), axis=1, keepdims=True)
+    row = jnp.sum(jnp.where(unit == me, row, 0), axis=1, keepdims=True)
     local = mine - unit * ROWS
     for r, low in extract(jnp.where((local >= 0) & (local < ROWS), local * 256 + row, BIG)):
         takes_ref[r : r + 1, 0:COUNT] = offset(jnp.where(low >= BIG, ROWS, low & 255))
@@ -72,8 +93,8 @@
             block[cell(at, r), :] = rows_ref[row_at(sends_ref[r, unit]), :]
 
 
-def pack_by_z_kernel(sends_ref, rows_ref, *blocks):
-    for dz, block in zip(Z_ORDER + (0,), blocks):
+def pack_by_z_kernel(shifts, sends_ref, rows_ref, *blocks):
+    for dz, block in zip(shifts, blocks):
         pack(sends_ref, rows_ref, block, [unit_at(line, dz, 1) for line in range(LINES)])
 
 
@@ -146,9 +167,9 @@
     return [blocks[-1]] + [blocks[order.index(i)] for i in range(1, 8)]
 
 
-def by_z(blocks):
+def by_z(blocks, order):
     blocks = list(blocks)
-    for dz in Z_ORDER:
+    for dz in order:
         blocks[dz] = sent(blocks[dz], 0, dz, 0)
     return blocks
 
@@ -184,21 +205,25 @@
     out = jax.ShapeDtypeStruct((FLAT, 128), jnp.float32)
     table = jax.ShapeDtypeStruct((8, 128), jnp.int32)
     sends, takes = call(tables_kernel, (table, table), [VMEM], (VMEM, VMEM), flops=2_000_000_000)(
-        perm.reshape(COUNT, ROWS).T
-    )
-    down = call(pack_by_z_kernel, PACKED, [SMEM, VMEM], (VMEM,) * 8)(sends, tiles_of(b_down))
-    down = by_z(in_order(down, Z_ORDER))
+        perm.reshape(COUNT * ROWS // 128, 128)
+    )
+    down = []
+    for shifts in (Z_ORDER[:2], Z_ORDER[2:] + (0,)):
+        down += call(
+            functools.partial(pack_by_z_kernel, shifts), PACKED[: len(shifts)], [SMEM, VMEM], (VMEM,) * len(shifts)
+        )(sends, tiles_of(b_down))
+    down = by_z(in_order(down, Z_ORDER), Z_ORDER)
     up = call(pack_by_line_kernel, PACKED, [SMEM, VMEM], (VMEM,) * 8)(sends, tiles_of(b_up))
     up = by_line(in_order(up, LINE_ORDER))
     up = call(turn_kernel, PACKED, [VMEM] * 8, (VMEM,) * 8)(*up)
-    up = by_z(up)
+    up = by_z(up, Z_LAST)
     down = call(turn_kernel, PACKED, [VMEM] * 8, (VMEM,) * 8)(*down)
     down = by_line(down)
     merged_down = call(
         unpack_by_line_kernel, out, [SMEM, VMEM] + [VMEM] * LINES, HBM, SCRATCH
     )(takes, tiles_of(a_down), *down)
-    late = Z_ORDER[-2:]
-    early = (0,) + Z_ORDER[:-2]
+    late = Z_LAST[-2:]
+    early = (0,) + Z_LAST[:-2]
     own = tiles_of(a_up)
     merged_up = call(
         functools.partial(unpack_early_kernel, early),

time: 194 us -> 182 us (0.938)
  waiting for transfers between devices: 113 us -> 94.1 us
  starting transfers between devices: 66.6 us -> 72.5 us
    ppermute x28, waiting for transfers between devices: 113 us -> 94.1 us  [sent(): return lax.ppermute(block, UNITS, pairs)]
    ppermute x28, starting transfers between devices: 66.6 us -> 72.5 us  [sent(): return lax.ppermute(block, UNITS, pairs)]
  transfers between devices with their start and end apart: 28 -> 28, of which waited for: 14 -> 14; matrix products, arithmetic and copies ran while one was open for 0% -> 0% of each run, Pallas kernels for 3% -> 4%
where the time goes in v1:
time: 182 us; the launch traced here: 181 us
  waiting for transfers between devices  94.1 us (52%)
  starting transfers between devices  72.5 us (40%)
  Pallas kernels  12.1 us (7%)
    ppermute x28, waiting for transfers between devices, sent(): return lax.ppermute(block, UNITS, pairs)  94.1 us
    ppermute x28, starting transfers between devices, sent(): return lax.ppermute(block, UNITS, pairs)  72.5 us
  transfers between devices with their start and end apart: 28, of which 14 were waited for; matrix products, arithmetic and copies ran while one was open for 0% of the time, Pallas kernels for 4%

profile of v1, /device:TPU:8, one launch (start us, length us, event | category | flops | bytes accessed | tf_op | source)
XLA Modules:
  0.0 181.0 jit_solution(6169085975882519462)
XLA Ops:
  3.8 4.7 %collective-permute-start.16 = (f32[640,128]{1,0:T(8,128)S(1)}, f32[640,128]{1,0:T(8,128)S(1)}, u32[]{:S(2)}, u32[]{:S(2)}) collective-permute-start(f32[640,128]{1,0:T(8,128)S(1)} %get-tuple-element.57), channel_id=1, source_target_pairs={{0,24},{4,28},{8,32},{12,36},{16,40},{20,44},{24,48},{28,52},{32,5... | collective-permute-start | bytes 983048 | tf_op jit(solution)/shard_map/ppermute | solution.py:163
  8.5 4.5 %collective-permute-start.17 = (f32[640,128]{1,0:T(8,128)S(1)}, f32[640,128]{1,0:T(8,128)S(1)}, u32[]{:S(2)}, u32[]{:S(2)}) collective-permute-start(f32[640,128]{1,0:T(8,128)S(1)} %get-tuple-element.58), channel_id=1, source_target_pairs={{0,32},{4,36},{8,40},{12,44},{16,48},{20,52},{24,56},{28,60},{32,0... | collective-permute-start | bytes 983048 | tf_op jit(solution)/shard_map/ppermute | solution.py:163
  14.8 4.9 %collective-permute-start.18 = (f32[640,128]{1,0:T(8,128)S(1)}, f32[640,128]{1,0:T(8,128)S(1)}, u32[]{:S(2)}, u32[]{:S(2)}) collective-permute-start(f32[640,128]{1,0:T(8,128)S(1)} %get-tuple-element.59), channel_id=1, source_target_pairs={{0,40},{4,44},{8,48},{12,52},{16,56},{20,60},{24,0},{28,4},{32,8},... | collective-permute-start | bytes 983048 | tf_op jit(solution)/shard_map/ppermute | solution.py:163
  21.1 11.0 %collective-permute-done.16.refs_3_ = f32[640,128]{1,0:T(8,128)S(1)} collective-permute-done((f32[640,128]{1,0:T(8,128)S(1)}, f32[640,128]{1,0:T(8,128)S(1)}, u32[]{:S(2)}, u32[]{:S(2)}) %collective-permute-start.16) | collective-permute-done | bytes 327712 | tf_op jit(solution)/shard_map/ppermute | solution.py:163
  32.1 19.1 %collective-permute-start.19 = (f32[640,128]{1,0:T(8,128)S(1)}, f32[640,128]{1,0:T(8,128)S(1)}, u32[]{:S(2)}, u32[]{:S(2)}) collective-permute-start(f32[640,128]{1,0:T(8,128)S(1)} %get-tuple-element.60), channel_id=1, source_target_pairs={{0,48},{4,52},{8,56},{12,60},{16,0},{20,4},{24,8},{28,12},{32,16},... | collective-permute-start | bytes 983048 | tf_op jit(solution)/shard_map/ppermute | solution.py:163
  51.2 2.2 %collective-permute-done.14.refs_1_ = f32[640,128]{1,0:T(8,128)S(1)} collective-permute-done((f32[640,128]{1,0:T(8,128)S(1)}, f32[640,128]{1,0:T(8,128)S(1)}, u32[]{:S(2)}, u32[]{:S(2)}) %collective-permute-start.14) | collective-permute-done | bytes 327712 | tf_op jit(solution)/shard_map/ppermute | solution.py:163
  53.4 11.9 %collective-permute-done.15.refs_2_ = f32[640,128]{1,0:T(8,128)S(1)} collective-permute-done((f32[640,128]{1,0:T(8,128)S(1)}, f32[640,128]{1,0:T(8,128)S(1)}, u32[]{:S(2)}, u32[]{:S(2)}) %collective-permute-start.15) | collective-permute-done | bytes 327712 | tf_op jit(solution)/shard_map/ppermute | solution.py:163
  65.4 1.5 collective-permute-start.1
  66.9 2.8 %collective-permute-start.3 = (f32[640,128]{1,0:T(8,128)S(1)}, f32[640,128]{1,0:T(8,128)S(1)}, u32[]{:S(2)}, u32[]{:S(2)}) collective-permute-start(f32[640,128]{1,0:T(8,128)S(1)} %get-tuple-element.42), channel_id=1, source_target_pairs={{0,128},{4,132},{8,136},{12,140},{16,144},{20,148},{24,152},{28,15... | collective-permute-start | bytes 983048 | tf_op jit(solution)/shard_map/ppermute | solution.py:163
  69.7 1.6 collective-permute-start.4
  71.3 1.7 collective-permute-start.5
  73.1 4.1 %collective-permute-done.1.refs_2_ = f32[640,128]{1,0:T(8,128)S(1)} collective-permute-done((f32[640,128]{1,0:T(8,128)S(1)}, f32[640,128]{1,0:T(8,128)S(1)}, u32[]{:S(2)}, u32[]{:S(2)}) %collective-permute-start.1) | collective-permute-done | bytes 327712 | tf_op jit(solution)/shard_map/ppermute | solution.py:163
  77.3 4.6 %collective-permute-done.2.refs_3_ = f32[640,128]{1,0:T(8,128)S(1)} collective-permute-done((f32[640,128]{1,0:T(8,128)S(1)}, f32[640,128]{1,0:T(8,128)S(1)}, u32[]{:S(2)}, u32[]{:S(2)}) %collective-permute-start.2) | collective-permute-done | bytes 327712 | tf_op jit(solution)/shard_map/ppermute | solution.py:163
  83.0 9.2 %collective-permute-done.3.refs_4_ = f32[640,128]{1,0:T(8,128)S(1)} collective-permute-done((f32[640,128]{1,0:T(8,128)S(1)}, f32[640,128]{1,0:T(8,128)S(1)}, u32[]{:S(2)}, u32[]{:S(2)}) %collective-permute-start.3) | collective-permute-done | bytes 327712 | tf_op jit(solution)/shard_map/ppermute | solution.py:163
  92.2 3.9 %collective-permute-done.4.refs_5_ = f32[640,128]{1,0:T(8,128)S(1)} collective-permute-done((f32[640,128]{1,0:T(8,128)S(1)}, f32[640,128]{1,0:T(8,128)S(1)}, u32[]{:S(2)}, u32[]{:S(2)}) %collective-permute-start.4) | collective-permute-done | bytes 327712 | tf_op jit(solution)/shard_map/ppermute | solution.py:163
  96.1 3.2 %collective-permute-done.6.refs_7_ = f32[640,128]{1,0:T(8,128)S(1)} collective-permute-done((f32[640,128]{1,0:T(8,128)S(1)}, f32[640,128]{1,0:T(8,128)S(1)}, u32[]{:S(2)}, u32[]{:S(2)}) %collective-permute-start.6) | collective-permute-done | bytes 327712 | tf_op jit(solution)/shard_map/ppermute | solution.py:163
  99.4 3.1 %collective-permute-start.7 = (f32[640,128]{1,0:T(8,128)S(1)}, f32[640,128]{1,0:T(8,128)S(1)}, u32[]{:S(2)}, u32[]{:S(2)}) collective-permute-start(f32[640,128]{1,0:T(8,128)S(1)} %get-tuple-element.47), channel_id=1, source_target_pairs={{0,8},{4,12},{8,16},{12,20},{16,24},{20,28},{24,32},{28,36},{32,40... | collective-permute-start | bytes 983048 | tf_op jit(solution)/shard_map/ppermute | solution.py:163
  102.7 1.4 collective-permute-start.9
  104.1 2.8 %collective-permute-start.10 = (f32[640,128]{1,0:T(8,128)S(1)}, f32[640,128]{1,0:T(8,128)S(1)}, u32[]{:S(2)}, u32[]{:S(2)}) collective-permute-start(f32[640,128]{1,0:T(8,128)S(1)} %get-tuple-element.50), channel_id=1, source_target_pairs={{0,48},{4,52},{8,56},{12,60},{16,0},{20,4},{24,8},{28,12},{32,16},... | collective-permute-start | bytes 983048 | tf_op jit(solution)/shard_map/ppermute | solution.py:163
  106.9 2.9 %collective-permute-start.11 = (f32[640,128]{1,0:T(8,128)S(1)}, f32[640,128]{1,0:T(8,128)S(1)}, u32[]{:S(2)}, u32[]{:S(2)}) collective-permute-start(f32[640,128]{1,0:T(8,128)S(1)} %get-tuple-element.51), channel_id=1, source_target_pairs={{0,24},{4,28},{8,32},{12,36},{16,40},{20,44},{24,48},{28,52},{32,5... | collective-permute-start | bytes 983048 | tf_op jit(solution)/shard_map/ppermute | solution.py:163
  109.7 2.7 %collective-permute-done.7.refs_1_ = f32[640,128]{1,0:T(8,128)S(1)} collective-permute-done((f32[640,128]{1,0:T(8,128)S(1)}, f32[640,128]{1,0:T(8,128)S(1)}, u32[]{:S(2)}, u32[]{:S(2)}) %collective-permute-start.7) | collective-permute-done | bytes 327712 | tf_op jit(solution)/shard_map/ppermute | solution.py:163
  112.4 12.1 %collective-permute-start.12 = (f32[640,128]{1,0:T(8,128)S(1)}, f32[640,128]{1,0:T(8,128)S(1)}, u32[]{:S(2)}, u32[]{:S(2)}) collective-permute-start(f32[640,128]{1,0:T(8,128)S(1)} %get-tuple-element.52), channel_id=1, source_target_pairs={{0,40},{4,44},{8,48},{12,52},{16,56},{20,60},{24,0},{28,4},{32,8},... | collective-permute-start | bytes 983048 | tf_op jit(solution)/shard_map/ppermute | solution.py:163
  124.5 3.1 %collective-permute-done.9.refs_3_ = f32[640,128]{1,0:T(8,128)S(1)} collective-permute-done((f32[640,128]{1,0:T(8,128)S(1)}, f32[640,128]{1,0:T(8,128)S(1)}, u32[]{:S(2)}, u32[]{:S(2)}) %collective-permute-start.9) | collective-permute-done | bytes 327712 | tf_op jit(solution)/shard_map/ppermute | solution.py:163
  128.8 2.6 %collective-permute-start.24 = (f32[640,128]{1,0:T(8,128)S(1)}, f32[640,128]{1,0:T(8,128)S(1)}, u32[]{:S(2)}, u32[]{:S(2)}) collective-permute-start(f32[640,128]{1,0:T(8,128)S(1)} %get-tuple-element.66), channel_id=1, source_target_pairs={{0,128},{4,132},{8,136},{12,140},{16,144},{20,148},{24,152},{28,15... | collective-permute-start | bytes 983048 | tf_op jit(solution)/shard_map/ppermute | solution.py:163
  131.4 21.3 %collective-permute-done.11.refs_5_ = f32[640,128]{1,0:T(8,128)S(1)} collective-permute-done((f32[640,128]{1,0:T(8,128)S(1)}, f32[640,128]{1,0:T(8,128)S(1)}, u32[]{:S(2)}, u32[]{:S(2)}) %collective-permute-start.11) | collective-permute-done | bytes 327712 | tf_op jit(solution)/shard_map/ppermute | solution.py:163
  152.8 2.5 %collective-permute-start.26 = (f32[640,128]{1,0:T(8,128)S(1)}, f32[640,128]{1,0:T(8,128)S(1)}, u32[]{:S(2)}, u32[]{:S(2)}) collective-permute-start(f32[640,128]{1,0:T(8,128)S(1)} %get-tuple-element.68), channel_id=1, source_target_pairs={{0,192},{4,196},{8,200},{12,204},{16,208},{20,212},{24,216},{28,22... | collective-permute-start | bytes 983048 | tf_op jit(solution)/shard_map/ppermute | solution.py:163
  155.3 8.9 %collective-permute-done.13.refs_1_ = f32[640,128]{1,0:T(8,128)S(1)} collective-permute-done((f32[640,128]{1,0:T(8,128)S(1)}, f32[640,128]{1,0:T(8,128)S(1)}, u32[]{:S(2)}, u32[]{:S(2)}) %collective-permute-start.13) | collective-permute-done | bytes 327712 | tf_op jit(solution)/shard_map/ppermute | solution.py:163
  164.2 1.6 collective-permute-start.27
  165.9 1.9 %shard_map.71.early_ref = f32[3712,128]{1,0:T(8,128)S(1)} custom-call(s32[8,128]{1,0:T(8,128)S(1)} %get-tuple-element.36.takes_ref, f32[3584,128]{1,0:T(8,128)S(1)} %bitcast.31, f32[640,128]{1,0:T(8,128)S(1)} %get-tuple-element.46.refs_0_, f32[640,128]{1,0:T(8,128)S(1)} %collective-permute-done.7.refs_1_, f32[640,128]{1,0:T(8,128)S(1)} %collective-permute-done.8.refs_2_, ...), custom_call_target="tpu_custom_call" | custom-call | flops 500000000 | bytes 1048576 | tf_op jit(solution)/shard_map/pallas_call | solution.py:228
  167.8 2.2 %shard_map.72 = f32[3584,128]{1,0:T(8,128)} custom-call(s32[8,128]{1,0:T(8,128)S(1)} %get-tuple-element.36.takes_ref, f32[3584,128]{1,0:T(8,128)S(1)} %bitcast.32, f32[3712,128]{1,0:T(8,128)S(1)} %shard_map.71.early_ref, f32[640,128]{1,0:T(8,128)S(1)} %collective-permute-done.12.refs_0_, f32[640,128]{1,0:T(8,128)S(1)} %collective-permute-done.13.refs_1_), custom_call_target="tpu_custom_call" | custom-call | flops 500000000 | bytes 1048576 | tf_op jit(solution)/shard_map/pallas_call | solution.py:234
  170.0 7.3 %collective-permute-done.27.refs_7_ = f32[640,128]{1,0:T(8,128)S(1)} collective-permute-done((f32[640,128]{1,0:T(8,128)S(1)}, f32[640,128]{1,0:T(8,128)S(1)}, u32[]{:S(2)}, u32[]{:S(2)}) %collective-permute-start.27) | collective-permute-done | bytes 327712 | tf_op jit(solution)/shard_map/ppermute | solution.py:163
  177.3 3.5 %shard_map.76 = f32[3584,128]{1,0:T(8,128)} custom-call(s32[8,128]{1,0:T(8,128)S(1)} %get-tuple-element.36.takes_ref, f32[3584,128]{1,0:T(8,128)S(1)} %bitcast.33, f32[640,128]{1,0:T(8,128)S(1)} %get-tuple-element.62.refs_0_, f32[640,128]{1,0:T(8,128)S(1)} %collective-permute-done.21.refs_1_, f32[640,128]{1,0:T(8,128)S(1)} %collective-permute-done.22.refs_2_, ...), custom_call_target="tpu_custom_call" | custom-call | flops 500000000 | bytes 1048576 | tf_op jit(solution)/shard_map/pallas_call | solution.py:222
  (43 shorter events, 9.2 us)
Async XLA Ops:
  1.4 1.5 copy-start.2
  3.0 16.8 %copy-start.3 = (f32[224,2048]{1,0:T(8,128)S(1)}, f32[224,2048]{1,0:T(8,128)}, u32[]{:S(2)}) copy-start(f32[224,2048]{1,0:T(8,128)} %param.7) | copy-start | bytes 5505028
  3.8 28.4 %collective-permute-start.16 = (f32[640,128]{1,0:T(8,128)S(1)}, f32[640,128]{1,0:T(8,128)S(1)}, u32[]{:S(2)}, u32[]{:S(2)}) collective-permute-start(f32[640,128]{1,0:T(8,128)S(1)} %get-tuple-element.57), channel_id=1, source_target_pairs={{0,24},{4,28},{8,32},{12,36},{16,40},{20,44},{24,48},{28,52},{32,5... | collective-permute-start | bytes 983048 | tf_op jit(solution)/shard_map/ppermute | solution.py:163
  8.5 42.8 %collective-permute-start.17 = (f32[640,128]{1,0:T(8,128)S(1)}, f32[640,128]{1,0:T(8,128)S(1)}, u32[]{:S(2)}, u32[]{:S(2)}) collective-permute-start(f32[640,128]{1,0:T(8,128)S(1)} %get-tuple-element.58), channel_id=1, source_target_pairs={{0,32},{4,36},{8,40},{12,44},{16,48},{20,52},{24,56},{28,60},{32,0... | collective-permute-start | bytes 983048 | tf_op jit(solution)/shard_map/ppermute | solution.py:163
  14.1 39.3 %collective-permute-start.14 = (f32[640,128]{1,0:T(8,128)S(1)}, f32[640,128]{1,0:T(8,128)S(1)}, u32[]{:S(2)}, u32[]{:S(2)}) collective-permute-start(f32[640,128]{1,0:T(8,128)S(1)} %get-tuple-element.55), channel_id=1, source_target_pairs={{0,8},{4,12},{8,16},{12,20},{16,24},{20,28},{24,32},{28,36},{32,40... | collective-permute-start | bytes 983048 | tf_op jit(solution)/shard_map/ppermute | solution.py:163
  14.2 51.2 %collective-permute-start.15 = (f32[640,128]{1,0:T(8,128)S(1)}, f32[640,128]{1,0:T(8,128)S(1)}, u32[]{:S(2)}, u32[]{:S(2)}) collective-permute-start(f32[640,128]{1,0:T(8,128)S(1)} %get-tuple-element.56), channel_id=1, source_target_pairs={{0,16},{4,20},{8,24},{12,28},{16,32},{20,36},{24,40},{28,44},{32,4... | collective-permute-start | bytes 983048 | tf_op jit(solution)/shard_map/ppermute | solution.py:163
  14.8 52.0 %collective-permute-start.18 = (f32[640,128]{1,0:T(8,128)S(1)}, f32[640,128]{1,0:T(8,128)S(1)}, u32[]{:S(2)}, u32[]{:S(2)}) collective-permute-start(f32[640,128]{1,0:T(8,128)S(1)} %get-tuple-element.59), channel_id=1, source_target_pairs={{0,40},{4,44},{8,48},{12,52},{16,56},{20,60},{24,0},{28,4},{32,8},... | collective-permute-start | bytes 983048 | tf_op jit(solution)/shard_map/ppermute | solution.py:163
  32.1 34.7 %collective-permute-start.19 = (f32[640,128]{1,0:T(8,128)S(1)}, f32[640,128]{1,0:T(8,128)S(1)}, u32[]{:S(2)}, u32[]{:S(2)}) collective-permute-start(f32[640,128]{1,0:T(8,128)S(1)} %get-tuple-element.60), channel_id=1, source_target_pairs={{0,48},{4,52},{8,56},{12,60},{16,0},{20,4},{24,8},{28,12},{32,16},... | collective-permute-start | bytes 983048 | tf_op jit(solution)/shard_map/ppermute | solution.py:163
  51.2 18.5 %collective-permute-start.20 = (f32[640,128]{1,0:T(8,128)S(1)}, f32[640,128]{1,0:T(8,128)S(1)}, u32[]{:S(2)}, u32[]{:S(2)}) collective-permute-start(f32[640,128]{1,0:T(8,128)S(1)} %get-tuple-element.61), channel_id=1, source_target_pairs={{0,56},{4,60},{8,0},{12,4},{16,8},{20,12},{24,16},{28,20},{32,24},... | collective-permute-start | bytes 983048 | tf_op jit(solution)/shard_map/ppermute | solution.py:163
  53.4 17.9 %collective-permute-start = (f32[640,128]{1,0:T(8,128)S(1)}, f32[640,128]{1,0:T(8,128)S(1)}, u32[]{:S(2)}, u32[]{:S(2)}) collective-permute-start(f32[640,128]{1,0:T(8,128)S(1)} %get-tuple-element.39), channel_id=1, source_target_pairs={{0,4},{4,0},{8,12},{12,8},{16,20},{20,16},{24,28},{28,24},{32,36},... | collective-permute-start | bytes 983048 | tf_op jit(solution)/shard_map/ppermute | solution.py:163
  65.4 11.8 %collective-permute-start.1 = (f32[640,128]{1,0:T(8,128)S(1)}, f32[640,128]{1,0:T(8,128)S(1)}, u32[]{:S(2)}, u32[]{:S(2)}) collective-permute-start(f32[640,128]{1,0:T(8,128)S(1)} %get-tuple-element.40), channel_id=1, source_target_pairs={{0,64},{4,68},{8,72},{12,76},{16,80},{20,84},{24,88},{28,92},{32,9... | collective-permute-start | bytes 983048 | tf_op jit(solution)/shard_map/ppermute | solution.py:163
  66.9 15.1 %collective-permute-start.2 = (f32[640,128]{1,0:T(8,128)S(1)}, f32[640,128]{1,0:T(8,128)S(1)}, u32[]{:S(2)}, u32[]{:S(2)}) collective-permute-start(f32[640,128]{1,0:T(8,128)S(1)} %get-tuple-element.41), channel_id=1, source_target_pairs={{0,68},{4,64},{8,76},{12,72},{16,84},{20,80},{24,92},{28,88},{32,1... | collective-permute-start | bytes 983048 | tf_op jit(solution)/shard_map/ppermute | solution.py:163
  66.9 25.3 %collective-permute-start.3 = (f32[640,128]{1,0:T(8,128)S(1)}, f32[640,128]{1,0:T(8,128)S(1)}, u32[]{:S(2)}, u32[]{:S(2)}) collective-permute-start(f32[640,128]{1,0:T(8,128)S(1)} %get-tuple-element.42), channel_id=1, source_target_pairs={{0,128},{4,132},{8,136},{12,140},{16,144},{20,148},{24,152},{28,15... | collective-permute-start | bytes 983048 | tf_op jit(solution)/shard_map/ppermute | solution.py:163
  69.7 26.4 %collective-permute-start.4 = (f32[640,128]{1,0:T(8,128)S(1)}, f32[640,128]{1,0:T(8,128)S(1)}, u32[]{:S(2)}, u32[]{:S(2)}) collective-permute-start(f32[640,128]{1,0:T(8,128)S(1)} %get-tuple-element.43), channel_id=1, source_target_pairs={{0,132},{4,128},{8,140},{12,136},{16,148},{20,144},{24,156},{28,15... | collective-permute-start | bytes 983048 | tf_op jit(solution)/shard_map/ppermute | solution.py:163
  71.3 24.7 %collective-permute-start.5 = (f32[640,128]{1,0:T(8,128)S(1)}, f32[640,128]{1,0:T(8,128)S(1)}, u32[]{:S(2)}, u32[]{:S(2)}) collective-permute-start(f32[640,128]{1,0:T(8,128)S(1)} %get-tuple-element.44), channel_id=1, source_target_pairs={{0,192},{4,196},{8,200},{12,204},{16,208},{20,212},{24,216},{28,22... | collective-permute-start | bytes 983048 | tf_op jit(solution)/shard_map/ppermute | solution.py:163
  77.1 22.1 %collective-permute-start.6 = (f32[640,128]{1,0:T(8,128)S(1)}, f32[640,128]{1,0:T(8,128)S(1)}, u32[]{:S(2)}, u32[]{:S(2)}) collective-permute-start(f32[640,128]{1,0:T(8,128)S(1)} %get-tuple-element.45), channel_id=1, source_target_pairs={{0,196},{4,192},{8,204},{12,200},{16,212},{20,208},{24,220},{28,21... | collective-permute-start | bytes 983048 | tf_op jit(solution)/shard_map/ppermute | solution.py:163
  77.3 88.6 %copy-start = (f32[224,2048]{1,0:T(8,128)S(1)}, f32[224,2048]{1,0:T(8,128)}, u32[]{:S(2)}) copy-start(f32[224,2048]{1,0:T(8,128)} %param.5) | copy-start | bytes 5505028
  82.0 22.1 %collective-permute-start.21 = (f32[640,128]{1,0:T(8,128)S(1)}, f32[640,128]{1,0:T(8,128)S(1)}, u32[]{:S(2)}, u32[]{:S(2)}) collective-permute-start(f32[640,128]{1,0:T(8,128)S(1)} %get-tuple-element.63), channel_id=1, source_target_pairs={{0,4},{4,0},{8,12},{12,8},{16,20},{20,16},{24,28},{28,24},{32,36},... | collective-permute-start | bytes 983048 | tf_op jit(solution)/shard_map/ppermute | solution.py:163
  92.2 14.7 %collective-permute-start.22 = (f32[640,128]{1,0:T(8,128)S(1)}, f32[640,128]{1,0:T(8,128)S(1)}, u32[]{:S(2)}, u32[]{:S(2)}) collective-permute-start(f32[640,128]{1,0:T(8,128)S(1)} %get-tuple-element.64), channel_id=1, source_target_pairs={{0,64},{4,68},{8,72},{12,76},{16,80},{20,84},{24,88},{28,92},{32,9... | collective-permute-start | bytes 983048 | tf_op jit(solution)/shard_map/ppermute | solution.py:163
  99.4 13.0 %collective-permute-start.7 = (f32[640,128]{1,0:T(8,128)S(1)}, f32[640,128]{1,0:T(8,128)S(1)}, u32[]{:S(2)}, u32[]{:S(2)}) collective-permute-start(f32[640,128]{1,0:T(8,128)S(1)} %get-tuple-element.47), channel_id=1, source_target_pairs={{0,8},{4,12},{8,16},{12,20},{16,24},{20,28},{24,32},{28,36},{32,40... | collective-permute-start | bytes 983048 | tf_op jit(solution)/shard_map/ppermute | solution.py:163
  102.5 21.9 %collective-permute-start.8 = (f32[640,128]{1,0:T(8,128)S(1)}, f32[640,128]{1,0:T(8,128)S(1)}, u32[]{:S(2)}, u32[]{:S(2)}) collective-permute-start(f32[640,128]{1,0:T(8,128)S(1)} %get-tuple-element.48), channel_id=1, source_target_pairs={{0,56},{4,60},{8,0},{12,4},{16,8},{20,12},{24,16},{28,20},{32,24},... | collective-permute-start | bytes 983048 | tf_op jit(solution)/shard_map/ppermute | solution.py:163
  102.7 24.8 %collective-permute-start.9 = (f32[640,128]{1,0:T(8,128)S(1)}, f32[640,128]{1,0:T(8,128)S(1)}, u32[]{:S(2)}, u32[]{:S(2)}) collective-permute-start(f32[640,128]{1,0:T(8,128)S(1)} %get-tuple-element.49), channel_id=1, source_target_pairs={{0,16},{4,20},{8,24},{12,28},{16,32},{20,36},{24,40},{28,44},{32,4... | collective-permute-start | bytes 983048 | tf_op jit(solution)/shard_map/ppermute | solution.py:163
  104.1 24.7 %collective-permute-start.10 = (f32[640,128]{1,0:T(8,128)S(1)}, f32[640,128]{1,0:T(8,128)S(1)}, u32[]{:S(2)}, u32[]{:S(2)}) collective-permute-start(f32[640,128]{1,0:T(8,128)S(1)} %get-tuple-element.50), channel_id=1, source_target_pairs={{0,48},{4,52},{8,56},{12,60},{16,0},{20,4},{24,8},{28,12},{32,16},... | collective-permute-start | bytes 983048 | tf_op jit(solution)/shard_map/ppermute | solution.py:163
  106.9 45.9 %collective-permute-start.11 = (f32[640,128]{1,0:T(8,128)S(1)}, f32[640,128]{1,0:T(8,128)S(1)}, u32[]{:S(2)}, u32[]{:S(2)}) collective-permute-start(f32[640,128]{1,0:T(8,128)S(1)} %get-tuple-element.51), channel_id=1, source_target_pairs={{0,24},{4,28},{8,32},{12,36},{16,40},{20,44},{24,48},{28,52},{32,5... | collective-permute-start | bytes 983048 | tf_op jit(solution)/shard_map/ppermute | solution.py:163
  112.4 40.4 %collective-permute-start.12 = (f32[640,128]{1,0:T(8,128)S(1)}, f32[640,128]{1,0:T(8,128)S(1)}, u32[]{:S(2)}, u32[]{:S(2)}) collective-permute-start(f32[640,128]{1,0:T(8,128)S(1)} %get-tuple-element.52), channel_id=1, source_target_pairs={{0,40},{4,44},{8,48},{12,52},{16,56},{20,60},{24,0},{28,4},{32,8},... | collective-permute-start | bytes 983048 | tf_op jit(solution)/shard_map/ppermute | solution.py:163
  124.5 39.8 %collective-permute-start.13 = (f32[640,128]{1,0:T(8,128)S(1)}, f32[640,128]{1,0:T(8,128)S(1)}, u32[]{:S(2)}, u32[]{:S(2)}) collective-permute-start(f32[640,128]{1,0:T(8,128)S(1)} %get-tuple-element.53), channel_id=1, source_target_pairs={{0,32},{4,36},{8,40},{12,44},{16,48},{20,52},{24,56},{28,60},{32,0... | collective-permute-start | bytes 983048 | tf_op jit(solution)/shard_map/ppermute | solution.py:163
  127.6 42.4 %collective-permute-start.23 = (f32[640,128]{1,0:T(8,128)S(1)}, f32[640,128]{1,0:T(8,128)S(1)}, u32[]{:S(2)}, u32[]{:S(2)}) collective-permute-start(f32[640,128]{1,0:T(8,128)S(1)} %get-tuple-element.65), channel_id=1, source_target_pairs={{0,68},{4,64},{8,76},{12,72},{16,84},{20,80},{24,92},{28,88},{32,1... | collective-permute-start | bytes 983048 | tf_op jit(solution)/shard_map/ppermute | solution.py:163
  128.8 41.2 %collective-permute-start.24 = (f32[640,128]{1,0:T(8,128)S(1)}, f32[640,128]{1,0:T(8,128)S(1)}, u32[]{:S(2)}, u32[]{:S(2)}) collective-permute-start(f32[640,128]{1,0:T(8,128)S(1)} %get-tuple-element.66), channel_id=1, source_target_pairs={{0,128},{4,132},{8,136},{12,140},{16,144},{20,148},{24,152},{28,15... | collective-permute-start | bytes 983048 | tf_op jit(solution)/shard_map/ppermute | solution.py:163
  152.8 17.2 %collective-permute-start.25 = (f32[640,128]{1,0:T(8,128)S(1)}, f32[640,128]{1,0:T(8,128)S(1)}, u32[]{:S(2)}, u32[]{:S(2)}) collective-permute-start(f32[640,128]{1,0:T(8,128)S(1)} %get-tuple-element.67), channel_id=1, source_target_pairs={{0,132},{4,128},{8,140},{12,136},{16,148},{20,144},{24,156},{28,15... | collective-permute-start | bytes 983048 | tf_op jit(solution)/shard_map/ppermute | solution.py:163
  152.8 17.2 %collective-permute-start.26 = (f32[640,128]{1,0:T(8,128)S(1)}, f32[640,128]{1,0:T(8,128)S(1)}, u32[]{:S(2)}, u32[]{:S(2)}) collective-permute-start(f32[640,128]{1,0:T(8,128)S(1)} %get-tuple-element.68), channel_id=1, source_target_pairs={{0,192},{4,196},{8,200},{12,204},{16,208},{20,212},{24,216},{28,22... | collective-permute-start | bytes 983048 | tf_op jit(solution)/shard_map/ppermute | solution.py:163
  164.2 13.1 %collective-permute-start.27 = (f32[640,128]{1,0:T(8,128)S(1)}, f32[640,128]{1,0:T(8,128)S(1)}, u32[]{:S(2)}, u32[]{:S(2)}) collective-permute-start(f32[640,128]{1,0:T(8,128)S(1)} %get-tuple-element.69), channel_id=1, source_target_pairs={{0,196},{4,192},{8,204},{12,200},{16,212},{20,208},{24,220},{28,21... | collective-permute-start | bytes 983048 | tf_op jit(solution)/shard_map/ppermute | solution.py:163
  167.8 9.6 %copy-start.1 = (f32[224,2048]{1,0:T(8,128)S(1)}, f32[224,2048]{1,0:T(8,128)}, u32[]{:S(2)}) copy-start(f32[224,2048]{1,0:T(8,128)} %param.6) | copy-start | bytes 5505028
  (1 other events, 0.8 us)

commit v2 on v1

--- a/solution.py
+++ b/solution.py
@@ -22,8 +22,9 @@
 CELL = LIMIT * TALL
 BLOCK = LINES * CELL
 BIG = 1 << 24
+STORES = 4
 Z_ORDER = (4, 3, 5, 2, 6, 1, 7)
-Z_LAST = (1, 7, 2, 6, 3, 5, 4)
+Z_LAST = (2, 6, 1, 7, 3, 5, 4)
 LINE_ORDER = (4, 2, 6, 5, 3, 7, 1)
 
 
@@ -45,12 +46,10 @@
         keys = jnp.where(keys == low, BIG, keys)
 
 
-def by_target(perm):
-    lines = COUNT * ROWS // 128
+def by_target(high, low):
+    lines = high.shape[0]
     line = lax.broadcasted_iota(jnp.int32, (lines, COUNT), 0)
     first = (lax.broadcasted_iota(jnp.int32, (lines, COUNT), 1) * ROWS) >> 7
-    high = (perm >> 7).astype(jnp.float32)
-    low = (perm & 127).astype(jnp.float32)
     parts = []
     for k in range(3):
         pick = jnp.where(line == first + k, 1.0, 0.0)
@@ -65,9 +64,9 @@
     return jnp.where((row >= 0) & (row < ROWS), whole, -1), row
 
 
-def tables_kernel(perm_ref, sends_ref, takes_ref):
+def tables_kernel(high_ref, low_ref, sends_ref, takes_ref):
     me = lax.axis_index(UNITS)
-    perm, row = by_target(perm_ref[...])
+    perm, row = by_target(high_ref[...], low_ref[...])
     unit = lax.broadcasted_iota(jnp.int32, perm.shape, 1)
     local = perm - me * ROWS
     for r, low in extract(jnp.where((local >= 0) & (local < ROWS), local, BIG)):
@@ -118,10 +117,16 @@
             merged[row_at(start), :] = (own + block[cell(at, r), :]) * 0.5
 
 
-def store(merged, out_ref, sem):
-    copy = pltpu.make_async_copy(merged.at[0:FLAT], out_ref, sem)
-    copy.start()
-    copy.wait()
+def store(merged, out_ref, sems):
+    part = FLAT // STORES
+    copies = [
+        pltpu.make_async_copy(merged.at[pl.ds(i * part, part)], out_ref.at[pl.ds(i * part, part)], sems.at[i])
+        for i in range(STORES)
+    ]
+    for copy in copies:
+        copy.start()
+    for copy in copies:
+        copy.wait()
 
 
 def unpack_by_line_kernel(takes_ref, own_ref, *refs):
@@ -139,7 +144,6 @@
 
 def unpack_late_kernel(shifts, takes_ref, own_ref, early_ref, *refs):
     blocks, (out_ref, merged, sem) = refs[: len(shifts)], refs[len(shifts) :]
-    merged[...] = early_ref[...]
     for dz, block in zip(shifts, blocks):
         merge(takes_ref, own_ref, block, merged, [unit_at(line, dz, -1) for line in range(LINES)])
     store(merged, out_ref, sem)
@@ -186,16 +190,18 @@
 HBM = pl.BlockSpec(memory_space=pltpu.HBM)
 PACKED = (jax.ShapeDtypeStruct((BLOCK, 128), jnp.float32),) * 8
 MERGED = (FLAT + 8 * TALL, 128)
-SCRATCH = [pltpu.VMEM(MERGED, jnp.float32), pltpu.SemaphoreType.DMA]
-
-
-def call(kernel, out, specs, out_specs, scratch=(), flops=500_000_000):
+SEMS = pltpu.SemaphoreType.DMA((STORES,))
+SCRATCH = [pltpu.VMEM(MERGED, jnp.float32), SEMS]
+
+
+def call(kernel, out, specs, out_specs, scratch=(), flops=500_000_000, aliases=None):
     return pl.pallas_call(
         kernel,
         out_shape=out,
         in_specs=specs,
         out_specs=out_specs,
         scratch_shapes=list(scratch),
+        input_output_aliases=aliases or {},
         cost_estimate=pl.CostEstimate(flops=flops, bytes_accessed=1 << 20, transcendentals=0),
         compiler_params=pltpu.CompilerParams(vmem_limit_bytes=12 << 20),
     )
@@ -204,11 +210,12 @@
 def on_device(a_up, a_down, b_up, b_down, perm):
     out = jax.ShapeDtypeStruct((FLAT, 128), jnp.float32)
     table = jax.ShapeDtypeStruct((8, 128), jnp.int32)
-    sends, takes = call(tables_kernel, (table, table), [VMEM], (VMEM, VMEM), flops=2_000_000_000)(
-        perm.reshape(COUNT * ROWS // 128, 128)
+    perm = perm.reshape(COUNT * ROWS // 128, 128)
+    sends, takes = call(tables_kernel, (table, table), [VMEM, VMEM], (VMEM, VMEM), flops=700_000_000)(
+        (perm >> 7).astype(jnp.float32), (perm & 127).astype(jnp.float32)
     )
     down = []
-    for shifts in (Z_ORDER[:2], Z_ORDER[2:] + (0,)):
+    for shifts in (Z_ORDER[:1], Z_ORDER[1:] + (0,)):
         down += call(
             functools.partial(pack_by_z_kernel, shifts), PACKED[: len(shifts)], [SMEM, VMEM], (VMEM,) * len(shifts)
         )(sends, tiles_of(b_down))
@@ -222,8 +229,8 @@
     merged_down = call(
         unpack_by_line_kernel, out, [SMEM, VMEM] + [VMEM] * LINES, HBM, SCRATCH
     )(takes, tiles_of(a_down), *down)
-    late = Z_LAST[-2:]
-    early = (0,) + Z_LAST[:-2]
+    late = Z_LAST[-1:]
+    early = (0,) + Z_LAST[:-1]
     own = tiles_of(a_up)
     merged_up = call(
         functools.partial(unpack_early_kernel, early),
@@ -231,8 +238,13 @@
         [SMEM, VMEM] + [VMEM] * len(early),
         VMEM,
     )(takes, own, *[up[dz] for dz in early])
-    merged_up = call(
-        functools.partial(unpack_late_kernel, late), out, [SMEM, VMEM, VMEM] + [VMEM] * len(late), HBM, SCRATCH
+    merged_up, _ = call(
+        functools.partial(unpack_late_kernel, late),
+        (out, jax.ShapeDtypeStruct(MERGED, jnp.float32)),
+        [SMEM, VMEM, VMEM] + [VMEM] * len(late),
+        (HBM, VMEM),
+        [SEMS],
+        aliases={2: 1},
     )(takes, own, merged_up, *[up[dz] for dz in late])
     return rows_of(merged_up), rows_of(merged_down)
 

time: 182 us -> 185 us (1.016)
  the two profiles are of different devices: /device:TPU:8 before, /device:TPU:199 now
where the time goes in v2:
time: 185 us
  waiting for transfers between devices  96.6 us (52%)
  starting transfers between devices  74.1 us (40%)
  Pallas kernels  12.1 us (7%)
    ppermute x28, waiting for transfers between devices, sent(): return lax.ppermute(block, UNITS, pairs)  96.6 us
    ppermute x28, starting transfers between devices, sent(): return lax.ppermute(block, UNITS, pairs)  74.1 us
  transfers between devices with their start and end apart: 28, of which 14 were waited for; matrix products, arithmetic and copies ran while one was open for 0% of the time, Pallas kernels for 3%

profile of v2, /device:TPU:199, one launch (start us, length us, event | category | flops | bytes accessed | tf_op | source)
XLA Modules:
  0.0 184.8 jit_solution(18369521554618798888)
XLA Ops:
  2.5 1.3 shard_map.69
  4.8 1.5 collective-permute-start.2
  6.2 1.8 collective-permute-start.3
  8.1 1.4 collective-permute-start.4
  9.5 1.2 shard_map.73
  11.1 2.6 %collective-permute-done.1.refs_2_ = f32[640,128]{1,0:T(8,128)S(1)} collective-permute-done((f32[640,128]{1,0:T(8,128)S(1)}, f32[640,128]{1,0:T(8,128)S(1)}, u32[]{:S(2)}, u32[]{:S(2)}) %collective-permute-start.1) | collective-permute-done | bytes 327712 | tf_op jit(solution)/shard_map/ppermute | solution.py:167
  13.8 1.9 %collective-permute-start.6 = (f32[640,128]{1,0:T(8,128)S(1)}, f32[640,128]{1,0:T(8,128)S(1)}, u32[]{:S(2)}, u32[]{:S(2)}) collective-permute-start(f32[640,128]{1,0:T(8,128)S(1)} %get-tuple-element.45), channel_id=1, source_target_pairs={{0,196},{4,192},{8,204},{12,200},{16,212},{20,208},{24,220},{28,21... | collective-permute-start | bytes 983048 | tf_op jit(solution)/shard_map/ppermute | solution.py:167
  15.7 6.2 %collective-permute-done.2.refs_3_ = f32[640,128]{1,0:T(8,128)S(1)} collective-permute-done((f32[640,128]{1,0:T(8,128)S(1)}, f32[640,128]{1,0:T(8,128)S(1)}, u32[]{:S(2)}, u32[]{:S(2)}) %collective-permute-start.2) | collective-permute-done | bytes 327712 | tf_op jit(solution)/shard_map/ppermute | solution.py:167
  22.6 2.2 %collective-permute-done.4.refs_5_ = f32[640,128]{1,0:T(8,128)S(1)} collective-permute-done((f32[640,128]{1,0:T(8,128)S(1)}, f32[640,128]{1,0:T(8,128)S(1)}, u32[]{:S(2)}, u32[]{:S(2)}) %collective-permute-start.4) | collective-permute-done | bytes 327712 | tf_op jit(solution)/shard_map/ppermute | solution.py:167
  24.8 1.8 collective-permute-start.16
  27.3 4.1 %collective-permute-done.5.refs_6_ = f32[640,128]{1,0:T(8,128)S(1)} collective-permute-done((f32[640,128]{1,0:T(8,128)S(1)}, f32[640,128]{1,0:T(8,128)S(1)}, u32[]{:S(2)}, u32[]{:S(2)}) %collective-permute-start.5) | collective-permute-done | bytes 327712 | tf_op jit(solution)/shard_map/ppermute | solution.py:167
  31.7 6.8 %collective-permute-done.6.refs_7_ = f32[640,128]{1,0:T(8,128)S(1)} collective-permute-done((f32[640,128]{1,0:T(8,128)S(1)}, f32[640,128]{1,0:T(8,128)S(1)}, u32[]{:S(2)}, u32[]{:S(2)}) %collective-permute-start.6) | collective-permute-done | bytes 327712 | tf_op jit(solution)/shard_map/ppermute | solution.py:167
  39.7 5.2 %collective-permute-done.15.refs_2_ = f32[640,128]{1,0:T(8,128)S(1)} collective-permute-done((f32[640,128]{1,0:T(8,128)S(1)}, f32[640,128]{1,0:T(8,128)S(1)}, u32[]{:S(2)}, u32[]{:S(2)}) %collective-permute-start.15) | collective-permute-done | bytes 327712 | tf_op jit(solution)/shard_map/ppermute | solution.py:167
  44.9 4.7 %collective-permute-start.20 = (f32[640,128]{1,0:T(8,128)S(1)}, f32[640,128]{1,0:T(8,128)S(1)}, u32[]{:S(2)}, u32[]{:S(2)}) collective-permute-start(f32[640,128]{1,0:T(8,128)S(1)} %get-tuple-element.61), channel_id=1, source_target_pairs={{0,56},{4,60},{8,0},{12,4},{16,8},{20,12},{24,16},{28,20},{32,24},... | collective-permute-start | bytes 983048 | tf_op jit(solution)/shard_map/ppermute | solution.py:167
  49.8 32.4 %collective-permute-done.16.refs_3_ = f32[640,128]{1,0:T(8,128)S(1)} collective-permute-done((f32[640,128]{1,0:T(8,128)S(1)}, f32[640,128]{1,0:T(8,128)S(1)}, u32[]{:S(2)}, u32[]{:S(2)}) %collective-permute-start.16) | collective-permute-done | bytes 327712 | tf_op jit(solution)/shard_map/ppermute | solution.py:167
  82.2 3.7 %collective-permute-start.8 = (f32[640,128]{1,0:T(8,128)S(1)}, f32[640,128]{1,0:T(8,128)S(1)}, u32[]{:S(2)}, u32[]{:S(2)}) collective-permute-start(f32[640,128]{1,0:T(8,128)S(1)} %get-tuple-element.48), channel_id=1, source_target_pairs={{0,48},{4,52},{8,56},{12,60},{16,0},{20,4},{24,8},{28,12},{32,16},... | collective-permute-start | bytes 983048 | tf_op jit(solution)/shard_map/ppermute | solution.py:167
  85.9 1.5 collective-permute-start.10
  87.4 2.5 %collective-permute-done.20.refs_7_ = f32[640,128]{1,0:T(8,128)S(1)} collective-permute-done((f32[640,128]{1,0:T(8,128)S(1)}, f32[640,128]{1,0:T(8,128)S(1)}, u32[]{:S(2)}, u32[]{:S(2)}) %collective-permute-start.20) | collective-permute-done | bytes 327712 | tf_op jit(solution)/shard_map/ppermute | solution.py:167
  89.9 5.6 %collective-permute-start.11 = (f32[640,128]{1,0:T(8,128)S(1)}, f32[640,128]{1,0:T(8,128)S(1)}, u32[]{:S(2)}, u32[]{:S(2)}) collective-permute-start(f32[640,128]{1,0:T(8,128)S(1)} %get-tuple-element.51), channel_id=1, source_target_pairs={{0,24},{4,28},{8,32},{12,36},{16,40},{20,44},{24,48},{28,52},{32,5... | collective-permute-start | bytes 983048 | tf_op jit(solution)/shard_map/ppermute | solution.py:167
  95.6 1.7 collective-permute-done.7.refs_1_
  97.3 8.7 %collective-permute-done.8.refs_2_ = f32[640,128]{1,0:T(8,128)S(1)} collective-permute-done((f32[640,128]{1,0:T(8,128)S(1)}, f32[640,128]{1,0:T(8,128)S(1)}, u32[]{:S(2)}, u32[]{:S(2)}) %collective-permute-start.8) | collective-permute-done | bytes 327712 | tf_op jit(solution)/shard_map/ppermute | solution.py:167
  106.0 1.1 collective-permute-start.13
  108.0 2.9 %collective-permute-done.10.refs_4_ = f32[640,128]{1,0:T(8,128)S(1)} collective-permute-done((f32[640,128]{1,0:T(8,128)S(1)}, f32[640,128]{1,0:T(8,128)S(1)}, u32[]{:S(2)}, u32[]{:S(2)}) %collective-permute-start.10) | collective-permute-done | bytes 327712 | tf_op jit(solution)/shard_map/ppermute | solution.py:167
  110.9 18.1 %collective-permute-start.22 = (f32[640,128]{1,0:T(8,128)S(1)}, f32[640,128]{1,0:T(8,128)S(1)}, u32[]{:S(2)}, u32[]{:S(2)}) collective-permute-start(f32[640,128]{1,0:T(8,128)S(1)} %get-tuple-element.64), channel_id=1, source_target_pairs={{0,64},{4,68},{8,72},{12,76},{16,80},{20,84},{24,88},{28,92},{32,9... | collective-permute-start | bytes 983048 | tf_op jit(solution)/shard_map/ppermute | solution.py:167
  129.1 23.3 %collective-permute-start.23 = (f32[640,128]{1,0:T(8,128)S(1)}, f32[640,128]{1,0:T(8,128)S(1)}, u32[]{:S(2)}, u32[]{:S(2)}) collective-permute-start(f32[640,128]{1,0:T(8,128)S(1)} %get-tuple-element.65), channel_id=1, source_target_pairs={{0,68},{4,64},{8,76},{12,72},{16,84},{20,80},{24,92},{28,88},{32,1... | collective-permute-start | bytes 983048 | tf_op jit(solution)/shard_map/ppermute | solution.py:167
  153.0 2.6 %collective-permute-start.27 = (f32[640,128]{1,0:T(8,128)S(1)}, f32[640,128]{1,0:T(8,128)S(1)}, u32[]{:S(2)}, u32[]{:S(2)}) collective-permute-start(f32[640,128]{1,0:T(8,128)S(1)} %get-tuple-element.69), channel_id=1, source_target_pairs={{0,196},{4,192},{8,204},{12,200},{16,212},{20,208},{24,220},{28,21... | collective-permute-start | bytes 983048 | tf_op jit(solution)/shard_map/ppermute | solution.py:167
  155.7 2.1 %shard_map.71.early_ref = f32[3712,128]{1,0:T(8,128)S(1)} custom-call(s32[8,128]{1,0:T(8,128)S(1)} %get-tuple-element.36.takes_ref, f32[3584,128]{1,0:T(8,128)S(1)} %bitcast.34, f32[640,128]{1,0:T(8,128)S(1)} %get-tuple-element.46.refs_0_, f32[640,128]{1,0:T(8,128)S(1)} %collective-permute-done.7.refs_1_, f32[640,128]{1,0:T(8,128)S(1)} %collective-permute-done.8.refs_2_, ...), custom_call_target="tpu_custom_call" | custom-call | flops 500000000 | bytes 1048576 | tf_op jit(solution)/shard_map/pallas_call | solution.py:235
  157.8 2.1 %shard_map.72 = (f32[3584,128]{1,0:T(8,128)}, f32[3712,128]{1,0:T(8,128)S(1)}) custom-call(s32[8,128]{1,0:T(8,128)S(1)} %get-tuple-element.36.takes_ref, f32[3584,128]{1,0:T(8,128)S(1)} %bitcast.35, f32[3712,128]{1,0:T(8,128)S(1)} %shard_map.71.early_ref, f32[640,128]{1,0:T(8,128)S(1)} %collective-permute-done.13.refs_0_), custom_call_target="tpu_custom_call", output_to_operand_aliasing={{1}: (2, {})} | custom-call | flops 500000000 | bytes 1048576 | tf_op jit(solution)/shard_map/pallas_call | solution.py:241
  159.8 7.1 %collective-permute-done.23.refs_3_ = f32[640,128]{1,0:T(8,128)S(1)} collective-permute-done((f32[640,128]{1,0:T(8,128)S(1)}, f32[640,128]{1,0:T(8,128)S(1)}, u32[]{:S(2)}, u32[]{:S(2)}) %collective-permute-start.23) | collective-permute-done | bytes 327712 | tf_op jit(solution)/shard_map/ppermute | solution.py:167
  166.9 7.1 %collective-permute-done.26.refs_6_ = f32[640,128]{1,0:T(8,128)S(1)} collective-permute-done((f32[640,128]{1,0:T(8,128)S(1)}, f32[640,128]{1,0:T(8,128)S(1)}, u32[]{:S(2)}, u32[]{:S(2)}) %collective-permute-start.26) | collective-permute-done | bytes 327712 | tf_op jit(solution)/shard_map/ppermute | solution.py:167
  174.0 7.0 %collective-permute-done.27.refs_7_ = f32[640,128]{1,0:T(8,128)S(1)} collective-permute-done((f32[640,128]{1,0:T(8,128)S(1)}, f32[640,128]{1,0:T(8,128)S(1)}, u32[]{:S(2)}, u32[]{:S(2)}) %collective-permute-start.27) | collective-permute-done | bytes 327712 | tf_op jit(solution)/shard_map/ppermute | solution.py:167
  181.0 3.5 %shard_map.76 = f32[3584,128]{1,0:T(8,128)} custom-call(s32[8,128]{1,0:T(8,128)S(1)} %get-tuple-element.36.takes_ref, f32[3584,128]{1,0:T(8,128)S(1)} %bitcast.38, f32[640,128]{1,0:T(8,128)S(1)} %get-tuple-element.62.refs_0_, f32[640,128]{1,0:T(8,128)S(1)} %collective-permute-done.21.refs_1_, f32[640,128]{1,0:T(8,128)S(1)} %collective-permute-done.22.refs_2_, ...), custom_call_target="tpu_custom_call" | custom-call | flops 500000000 | bytes 1048576 | tf_op jit(solution)/shard_map/pallas_call | solution.py:229
  (42 shorter events, 8.0 us)
Async XLA Ops:
  0.6 1.8 copy-start.3
  1.6 7.9 %copy-start.1 = (f32[224,2048]{1,0:T(8,128)S(1)}, f32[224,2048]{1,0:T(8,128)}, u32[]{:S(2)}) copy-start(f32[224,2048]{1,0:T(8,128)} %param.8) | copy-start | bytes 5505028
  3.8 6.9 %collective-permute-start = (f32[640,128]{1,0:T(8,128)S(1)}, f32[640,128]{1,0:T(8,128)S(1)}, u32[]{:S(2)}, u32[]{:S(2)}) collective-permute-start(f32[640,128]{1,0:T(8,128)S(1)} %get-tuple-element.39), channel_id=1, source_target_pairs={{0,4},{4,0},{8,12},{12,8},{16,20},{20,16},{24,28},{28,24},{32,36},... | collective-permute-start | bytes 983048 | tf_op jit(solution)/shard_map/ppermute | solution.py:167
  4.6 9.2 %collective-permute-start.1 = (f32[640,128]{1,0:T(8,128)S(1)}, f32[640,128]{1,0:T(8,128)S(1)}, u32[]{:S(2)}, u32[]{:S(2)}) collective-permute-start(f32[640,128]{1,0:T(8,128)S(1)} %get-tuple-element.40), channel_id=1, source_target_pairs={{0,64},{4,68},{8,72},{12,76},{16,80},{20,84},{24,88},{28,92},{32,9... | collective-permute-start | bytes 983048 | tf_op jit(solution)/shard_map/ppermute | solution.py:167
  4.8 17.1 %collective-permute-start.2 = (f32[640,128]{1,0:T(8,128)S(1)}, f32[640,128]{1,0:T(8,128)S(1)}, u32[]{:S(2)}, u32[]{:S(2)}) collective-permute-start(f32[640,128]{1,0:T(8,128)S(1)} %get-tuple-element.41), channel_id=1, source_target_pairs={{0,68},{4,64},{8,76},{12,72},{16,84},{20,80},{24,92},{28,88},{32,1... | collective-permute-start | bytes 983048 | tf_op jit(solution)/shard_map/ppermute | solution.py:167
  6.2 16.4 %collective-permute-start.3 = (f32[640,128]{1,0:T(8,128)S(1)}, f32[640,128]{1,0:T(8,128)S(1)}, u32[]{:S(2)}, u32[]{:S(2)}) collective-permute-start(f32[640,128]{1,0:T(8,128)S(1)} %get-tuple-element.42), channel_id=1, source_target_pairs={{0,128},{4,132},{8,136},{12,140},{16,144},{20,148},{24,152},{28,15... | collective-permute-start | bytes 983048 | tf_op jit(solution)/shard_map/ppermute | solution.py:167
  8.1 16.8 %collective-permute-start.4 = (f32[640,128]{1,0:T(8,128)S(1)}, f32[640,128]{1,0:T(8,128)S(1)}, u32[]{:S(2)}, u32[]{:S(2)}) collective-permute-start(f32[640,128]{1,0:T(8,128)S(1)} %get-tuple-element.43), channel_id=1, source_target_pairs={{0,132},{4,128},{8,140},{12,136},{16,148},{20,144},{24,156},{28,15... | collective-permute-start | bytes 983048 | tf_op jit(solution)/shard_map/ppermute | solution.py:167
  10.8 20.7 %collective-permute-start.5 = (f32[640,128]{1,0:T(8,128)S(1)}, f32[640,128]{1,0:T(8,128)S(1)}, u32[]{:S(2)}, u32[]{:S(2)}) collective-permute-start(f32[640,128]{1,0:T(8,128)S(1)} %get-tuple-element.44), channel_id=1, source_target_pairs={{0,192},{4,196},{8,200},{12,204},{16,208},{20,212},{24,216},{28,22... | collective-permute-start | bytes 983048 | tf_op jit(solution)/shard_map/ppermute | solution.py:167
  13.8 24.7 %collective-permute-start.6 = (f32[640,128]{1,0:T(8,128)S(1)}, f32[640,128]{1,0:T(8,128)S(1)}, u32[]{:S(2)}, u32[]{:S(2)}) collective-permute-start(f32[640,128]{1,0:T(8,128)S(1)} %get-tuple-element.45), channel_id=1, source_target_pairs={{0,196},{4,192},{8,204},{12,200},{16,212},{20,208},{24,220},{28,21... | collective-permute-start | bytes 983048 | tf_op jit(solution)/shard_map/ppermute | solution.py:167
  21.9 17.3 %collective-permute-start.14 = (f32[640,128]{1,0:T(8,128)S(1)}, f32[640,128]{1,0:T(8,128)S(1)}, u32[]{:S(2)}, u32[]{:S(2)}) collective-permute-start(f32[640,128]{1,0:T(8,128)S(1)} %get-tuple-element.56), channel_id=1, source_target_pairs={{0,8},{4,12},{8,16},{12,20},{16,24},{20,28},{24,32},{28,36},{32,40... | collective-permute-start | bytes 983048 | tf_op jit(solution)/shard_map/ppermute | solution.py:167
  22.6 22.3 %collective-permute-start.15 = (f32[640,128]{1,0:T(8,128)S(1)}, f32[640,128]{1,0:T(8,128)S(1)}, u32[]{:S(2)}, u32[]{:S(2)}) collective-permute-start(f32[640,128]{1,0:T(8,128)S(1)} %get-tuple-element.57), channel_id=1, source_target_pairs={{0,16},{4,20},{8,24},{12,28},{16,32},{20,36},{24,40},{28,44},{32,4... | collective-permute-start | bytes 983048 | tf_op jit(solution)/shard_map/ppermute | solution.py:167
  24.8 57.4 %collective-permute-start.16 = (f32[640,128]{1,0:T(8,128)S(1)}, f32[640,128]{1,0:T(8,128)S(1)}, u32[]{:S(2)}, u32[]{:S(2)}) collective-permute-start(f32[640,128]{1,0:T(8,128)S(1)} %get-tuple-element.58), channel_id=1, source_target_pairs={{0,24},{4,28},{8,32},{12,36},{16,40},{20,44},{24,48},{28,52},{32,5... | collective-permute-start | bytes 983048 | tf_op jit(solution)/shard_map/ppermute | solution.py:167
  31.5 50.7 %collective-permute-start.17 = (f32[640,128]{1,0:T(8,128)S(1)}, f32[640,128]{1,0:T(8,128)S(1)}, u32[]{:S(2)}, u32[]{:S(2)}) collective-permute-start(f32[640,128]{1,0:T(8,128)S(1)} %shard_map.74), channel_id=1, source_target_pairs={{0,32},{4,36},{8,40},{12,44},{16,48},{20,52},{24,56},{28,60},{32,0... | collective-permute-start | bytes 983048 | tf_op jit(solution)/shard_map/ppermute | solution.py:167
  38.5 47.4 %collective-permute-start.18 = (f32[640,128]{1,0:T(8,128)S(1)}, f32[640,128]{1,0:T(8,128)S(1)}, u32[]{:S(2)}, u32[]{:S(2)}) collective-permute-start(f32[640,128]{1,0:T(8,128)S(1)} %get-tuple-element.59), channel_id=1, source_target_pairs={{0,40},{4,44},{8,48},{12,52},{16,56},{20,60},{24,0},{28,4},{32,8},... | collective-permute-start | bytes 983048 | tf_op jit(solution)/shard_map/ppermute | solution.py:167
  39.2 46.7 %collective-permute-start.19 = (f32[640,128]{1,0:T(8,128)S(1)}, f32[640,128]{1,0:T(8,128)S(1)}, u32[]{:S(2)}, u32[]{:S(2)}) collective-permute-start(f32[640,128]{1,0:T(8,128)S(1)} %get-tuple-element.60), channel_id=1, source_target_pairs={{0,48},{4,52},{8,56},{12,60},{16,0},{20,4},{24,8},{28,12},{32,16},... | collective-permute-start | bytes 983048 | tf_op jit(solution)/shard_map/ppermute | solution.py:167
  44.9 44.9 %collective-permute-start.20 = (f32[640,128]{1,0:T(8,128)S(1)}, f32[640,128]{1,0:T(8,128)S(1)}, u32[]{:S(2)}, u32[]{:S(2)}) collective-permute-start(f32[640,128]{1,0:T(8,128)S(1)} %get-tuple-element.61), channel_id=1, source_target_pairs={{0,56},{4,60},{8,0},{12,4},{16,8},{20,12},{24,16},{28,20},{32,24},... | collective-permute-start | bytes 983048 | tf_op jit(solution)/shard_map/ppermute | solution.py:167
  49.8 105.9 %copy-start = (f32[224,2048]{1,0:T(8,128)S(1)}, f32[224,2048]{1,0:T(8,128)}, u32[]{:S(2)}) copy-start(f32[224,2048]{1,0:T(8,128)} %param.5) | copy-start | bytes 5505028
  82.2 15.1 %collective-permute-start.7 = (f32[640,128]{1,0:T(8,128)S(1)}, f32[640,128]{1,0:T(8,128)S(1)}, u32[]{:S(2)}, u32[]{:S(2)}) collective-permute-start(f32[640,128]{1,0:T(8,128)S(1)} %get-tuple-element.47), channel_id=1, source_target_pairs={{0,16},{4,20},{8,24},{12,28},{16,32},{20,36},{24,40},{28,44},{32,4... | collective-permute-start | bytes 983048 | tf_op jit(solution)/shard_map/ppermute | solution.py:167
  82.2 23.8 %collective-permute-start.8 = (f32[640,128]{1,0:T(8,128)S(1)}, f32[640,128]{1,0:T(8,128)S(1)}, u32[]{:S(2)}, u32[]{:S(2)}) collective-permute-start(f32[640,128]{1,0:T(8,128)S(1)} %get-tuple-element.48), channel_id=1, source_target_pairs={{0,48},{4,52},{8,56},{12,60},{16,0},{20,4},{24,8},{28,12},{32,16},... | collective-permute-start | bytes 983048 | tf_op jit(solution)/shard_map/ppermute | solution.py:167
  85.9 21.2 %collective-permute-start.9 = (f32[640,128]{1,0:T(8,128)S(1)}, f32[640,128]{1,0:T(8,128)S(1)}, u32[]{:S(2)}, u32[]{:S(2)}) collective-permute-start(f32[640,128]{1,0:T(8,128)S(1)} %get-tuple-element.49), channel_id=1, source_target_pairs={{0,8},{4,12},{8,16},{12,20},{16,24},{20,28},{24,32},{28,36},{32,40... | collective-permute-start | bytes 983048 | tf_op jit(solution)/shard_map/ppermute | solution.py:167
  85.9 25.0 %collective-permute-start.10 = (f32[640,128]{1,0:T(8,128)S(1)}, f32[640,128]{1,0:T(8,128)S(1)}, u32[]{:S(2)}, u32[]{:S(2)}) collective-permute-start(f32[640,128]{1,0:T(8,128)S(1)} %get-tuple-element.50), channel_id=1, source_target_pairs={{0,56},{4,60},{8,0},{12,4},{16,8},{20,12},{24,16},{28,20},{32,24},... | collective-permute-start | bytes 983048 | tf_op jit(solution)/shard_map/ppermute | solution.py:167
  89.9 39.2 %collective-permute-start.11 = (f32[640,128]{1,0:T(8,128)S(1)}, f32[640,128]{1,0:T(8,128)S(1)}, u32[]{:S(2)}, u32[]{:S(2)}) collective-permute-start(f32[640,128]{1,0:T(8,128)S(1)} %get-tuple-element.51), channel_id=1, source_target_pairs={{0,24},{4,28},{8,32},{12,36},{16,40},{20,44},{24,48},{28,52},{32,5... | collective-permute-start | bytes 983048 | tf_op jit(solution)/shard_map/ppermute | solution.py:167
  97.3 55.0 %collective-permute-start.12 = (f32[640,128]{1,0:T(8,128)S(1)}, f32[640,128]{1,0:T(8,128)S(1)}, u32[]{:S(2)}, u32[]{:S(2)}) collective-permute-start(f32[640,128]{1,0:T(8,128)S(1)} %get-tuple-element.52), channel_id=1, source_target_pairs={{0,40},{4,44},{8,48},{12,52},{16,56},{20,60},{24,0},{28,4},{32,8},... | collective-permute-start | bytes 983048 | tf_op jit(solution)/shard_map/ppermute | solution.py:167
  106.0 46.3 %collective-permute-start.13 = (f32[640,128]{1,0:T(8,128)S(1)}, f32[640,128]{1,0:T(8,128)S(1)}, u32[]{:S(2)}, u32[]{:S(2)}) collective-permute-start(f32[640,128]{1,0:T(8,128)S(1)} %get-tuple-element.53), channel_id=1, source_target_pairs={{0,32},{4,36},{8,40},{12,44},{16,48},{20,52},{24,56},{28,60},{32,0... | collective-permute-start | bytes 983048 | tf_op jit(solution)/shard_map/ppermute | solution.py:167
  107.1 45.3 %collective-permute-start.21 = (f32[640,128]{1,0:T(8,128)S(1)}, f32[640,128]{1,0:T(8,128)S(1)}, u32[]{:S(2)}, u32[]{:S(2)}) collective-permute-start(f32[640,128]{1,0:T(8,128)S(1)} %get-tuple-element.63), channel_id=1, source_target_pairs={{0,4},{4,0},{8,12},{12,8},{16,20},{20,16},{24,28},{28,24},{32,36},... | collective-permute-start | bytes 983048 | tf_op jit(solution)/shard_map/ppermute | solution.py:167
  110.9 42.1 %collective-permute-start.22 = (f32[640,128]{1,0:T(8,128)S(1)}, f32[640,128]{1,0:T(8,128)S(1)}, u32[]{:S(2)}, u32[]{:S(2)}) collective-permute-start(f32[640,128]{1,0:T(8,128)S(1)} %get-tuple-element.64), channel_id=1, source_target_pairs={{0,64},{4,68},{8,72},{12,76},{16,80},{20,84},{24,88},{28,92},{32,9... | collective-permute-start | bytes 983048 | tf_op jit(solution)/shard_map/ppermute | solution.py:167
  129.1 37.8 %collective-permute-start.23 = (f32[640,128]{1,0:T(8,128)S(1)}, f32[640,128]{1,0:T(8,128)S(1)}, u32[]{:S(2)}, u32[]{:S(2)}) collective-permute-start(f32[640,128]{1,0:T(8,128)S(1)} %get-tuple-element.65), channel_id=1, source_target_pairs={{0,68},{4,64},{8,76},{12,72},{16,84},{20,80},{24,92},{28,88},{32,1... | collective-permute-start | bytes 983048 | tf_op jit(solution)/shard_map/ppermute | solution.py:167
  152.3 14.6 %collective-permute-start.24 = (f32[640,128]{1,0:T(8,128)S(1)}, f32[640,128]{1,0:T(8,128)S(1)}, u32[]{:S(2)}, u32[]{:S(2)}) collective-permute-start(f32[640,128]{1,0:T(8,128)S(1)} %get-tuple-element.66), channel_id=1, source_target_pairs={{0,128},{4,132},{8,136},{12,140},{16,144},{20,148},{24,152},{28,15... | collective-permute-start | bytes 983048 | tf_op jit(solution)/shard_map/ppermute | solution.py:167
  152.4 14.5 %collective-permute-start.25 = (f32[640,128]{1,0:T(8,128)S(1)}, f32[640,128]{1,0:T(8,128)S(1)}, u32[]{:S(2)}, u32[]{:S(2)}) collective-permute-start(f32[640,128]{1,0:T(8,128)S(1)} %get-tuple-element.67), channel_id=1, source_target_pairs={{0,132},{4,128},{8,140},{12,136},{16,148},{20,144},{24,156},{28,15... | collective-permute-start | bytes 983048 | tf_op jit(solution)/shard_map/ppermute | solution.py:167
  152.5 21.6 %collective-permute-start.26 = (f32[640,128]{1,0:T(8,128)S(1)}, f32[640,128]{1,0:T(8,128)S(1)}, u32[]{:S(2)}, u32[]{:S(2)}) collective-permute-start(f32[640,128]{1,0:T(8,128)S(1)} %get-tuple-element.68), channel_id=1, source_target_pairs={{0,192},{4,196},{8,200},{12,204},{16,208},{20,212},{24,216},{28,22... | collective-permute-start | bytes 983048 | tf_op jit(solution)/shard_map/ppermute | solution.py:167
  153.0 28.0 %collective-permute-start.27 = (f32[640,128]{1,0:T(8,128)S(1)}, f32[640,128]{1,0:T(8,128)S(1)}, u32[]{:S(2)}, u32[]{:S(2)}) collective-permute-start(f32[640,128]{1,0:T(8,128)S(1)} %get-tuple-element.69), channel_id=1, source_target_pairs={{0,196},{4,192},{8,204},{12,200},{16,212},{20,208},{24,220},{28,21... | collective-permute-start | bytes 983048 | tf_op jit(solution)/shard_map/ppermute | solution.py:167
  157.7 23.3 %copy-start.2 = (f32[224,2048]{1,0:T(8,128)S(1)}, f32[224,2048]{1,0:T(8,128)}, u32[]{:S(2)}) copy-start(f32[224,2048]{1,0:T(8,128)} %param.6) | copy-start | bytes 5505028

commit v3 on v2

--- a/solution.py
+++ b/solution.py
@@ -26,6 +26,9 @@
 Z_ORDER = (4, 3, 5, 2, 6, 1, 7)
 Z_LAST = (2, 6, 1, 7, 3, 5, 4)
 LINE_ORDER = (4, 2, 6, 5, 3, 7, 1)
+LAST = Z_LAST[-1]
+EARLY = (0,) + Z_LAST[:-1]
+HALF = TALL // 2
 
 
 def unit_at(line, dz, sign):
@@ -86,6 +89,10 @@
     return slice(at * CELL + r * TALL, at * CELL + r * TALL + TALL)
 
 
+def half_cell(at, r):
+    return slice((at * LIMIT + r) * HALF, (at * LIMIT + r + 1) * HALF)
+
+
 def pack(sends_ref, rows_ref, block, units):
     for at, unit in enumerate(units):
         for r in range(LIMIT):
@@ -107,6 +114,17 @@
     for i in range(8):
         for j in range(8):
             targets[j][i * CELL : (i + 1) * CELL, :] = sources[i][j * CELL : (j + 1) * CELL, :]
+
+
+def turn_split_kernel(*refs):
+    sources, targets, halves = refs[:8], refs[8:15], refs[15:]
+    for i in range(8):
+        for target, j in zip(targets, EARLY):
+            target[i * CELL : (i + 1) * CELL, :] = sources[i][j * CELL : (j + 1) * CELL, :]
+        for r in range(LIMIT):
+            for side, half in enumerate(halves):
+                at = LAST * CELL + r * TALL + side * HALF
+                half[half_cell(i, r), :] = sources[i][at : at + HALF, :]
 
 
 def merge(takes_ref, own_ref, block, merged, units):
@@ -142,11 +160,22 @@
         merge(takes_ref, own_ref, block, merged, [unit_at(line, dz, -1) for line in range(LINES)])
 
 
-def unpack_late_kernel(shifts, takes_ref, own_ref, early_ref, *refs):
-    blocks, (out_ref, merged, sem) = refs[: len(shifts)], refs[len(shifts) :]
-    for dz, block in zip(shifts, blocks):
-        merge(takes_ref, own_ref, block, merged, [unit_at(line, dz, -1) for line in range(LINES)])
-    store(merged, out_ref, sem)
+def unpack_half_kernel(side, takes_ref, own_ref, early_ref, block, *refs):
+    out_ref, merged, sems = refs[-3:]
+    shift = side * HALF * 8
+    for line in range(LINES):
+        unit = unit_at(line, LAST, -1)
+        for r in range(LIMIT):
+            start = takes_ref[r, unit]
+            own = own_ref[pl.ds(jnp.where(start < FLAT, start, 0) + shift, HALF, stride=8), :]
+            merged[pl.ds(start + shift, HALF, stride=8), :] = (own + block[half_cell(line, r), :]) * 0.5
+    copies = []
+    for group in range(ROWS // 8):
+        rows = pl.ds(group * 8 * TALL + shift, 8 * HALF)
+        copies.append(pltpu.make_async_copy(merged.at[rows], out_ref.at[rows], sems.at[group]))
+        copies[-1].start()
+    for copy in copies:
+        copy.wait()
 
 
 def tiles_of(x):
@@ -172,7 +201,7 @@
 
 
 def by_z(blocks, order):
-    blocks = list(blocks)
+    blocks = dict(blocks) if isinstance(blocks, dict) else list(blocks)
     for dz in order:
         blocks[dz] = sent(blocks[dz], 0, dz, 0)
     return blocks
@@ -222,30 +251,38 @@
     down = by_z(in_order(down, Z_ORDER), Z_ORDER)
     up = call(pack_by_line_kernel, PACKED, [SMEM, VMEM], (VMEM,) * 8)(sends, tiles_of(b_up))
     up = by_line(in_order(up, LINE_ORDER))
-    up = call(turn_kernel, PACKED, [VMEM] * 8, (VMEM,) * 8)(*up)
-    up = by_z(up, Z_LAST)
+    half = jax.ShapeDtypeStruct((BLOCK // 2, 128), jnp.float32)
+    *up, left, right = call(turn_split_kernel, PACKED[:7] + (half, half), [VMEM] * 8, (VMEM,) * 9)(*up)
+    up = by_z(dict(zip(EARLY, up)), EARLY[1:])
+    left = sent(left, 0, LAST, 0)
+    right = sent(right, 0, LAST, 0)
     down = call(turn_kernel, PACKED, [VMEM] * 8, (VMEM,) * 8)(*down)
     down = by_line(down)
     merged_down = call(
         unpack_by_line_kernel, out, [SMEM, VMEM] + [VMEM] * LINES, HBM, SCRATCH
     )(takes, tiles_of(a_down), *down)
-    late = Z_LAST[-1:]
-    early = (0,) + Z_LAST[:-1]
     own = tiles_of(a_up)
-    merged_up = call(
-        functools.partial(unpack_early_kernel, early),
-        jax.ShapeDtypeStruct(MERGED, jnp.float32),
-        [SMEM, VMEM] + [VMEM] * len(early),
-        VMEM,
-    )(takes, own, *[up[dz] for dz in early])
+    merged = jax.ShapeDtypeStruct(MERGED, jnp.float32)
+    rows = call(
+        functools.partial(unpack_early_kernel, EARLY), merged, [SMEM, VMEM] + [VMEM] * len(EARLY), VMEM
+    )(takes, own, *[up[dz] for dz in EARLY])
+    stores = [pltpu.SemaphoreType.DMA((ROWS // 8,))]
+    merged_up, rows = call(
+        functools.partial(unpack_half_kernel, 0),
+        (out, merged),
+        [SMEM, VMEM, VMEM, VMEM],
+        (HBM, VMEM),
+        stores,
+        aliases={2: 1},
+    )(takes, own, rows, left)
     merged_up, _ = call(
-        functools.partial(unpack_late_kernel, late),
-        (out, jax.ShapeDtypeStruct(MERGED, jnp.float32)),
-        [SMEM, VMEM, VMEM] + [VMEM] * len(late),
+        functools.partial(unpack_half_kernel, 1),
+        (out, merged),
+        [SMEM, VMEM, VMEM, VMEM, HBM],
         (HBM, VMEM),
-        [SEMS],
-        aliases={2: 1},
-    )(takes, own, merged_up, *[up[dz] for dz in late])
+        stores,
+        aliases={2: 1, 4: 0},
+    )(takes, own, rows, right, merged_up)
     return rows_of(merged_up), rows_of(merged_down)
 
 

time: 185 us -> 188 us (1.016)
  the two profiles are of different devices: /device:TPU:199 before, /device:TPU:8 now
where the time goes in v3:
time: 188 us; the launch traced here: 186 us
  waiting for transfers between devices  99.7 us (53%)
  starting transfers between devices  70.6 us (38%)
  Pallas kernels  14 us (7%)
    ppermute x29, waiting for transfers between devices, sent(): return lax.ppermute(block, UNITS, pairs)  99.7 us
    ppermute x29, starting transfers between devices, sent(): return lax.ppermute(block, UNITS, pairs)  70.6 us
  transfers between devices with their start and end apart: 29, of which 15 were waited for; matrix products, arithmetic and copies ran while one was open for 0% of the time, Pallas kernels for 4%

profile of v3, /device:TPU:8, one launch (start us, length us, event | category | flops | bytes accessed | tf_op | source)
XLA Modules:
  0.0 186.2 jit_solution(6772439898983405438)
XLA Ops:
  3.9 1.6 collective-permute-start.1
  6.7 1.7 collective-permute-start.3
  10.0 1.7 collective-permute-start.5
  11.7 4.1 %collective-permute-done.1.refs_2_ = f32[640,128]{1,0:T(8,128)S(1)} collective-permute-done((f32[640,128]{1,0:T(8,128)S(1)}, f32[640,128]{1,0:T(8,128)S(1)}, u32[]{:S(2)}, u32[]{:S(2)}) %collective-permute-start.1) | collective-permute-done | bytes 327712 | tf_op jit(solution)/shard_map/ppermute | solution.py:196
  17.2 4.5 %collective-permute-done.2.refs_3_ = f32[640,128]{1,0:T(8,128)S(1)} collective-permute-done((f32[640,128]{1,0:T(8,128)S(1)}, f32[640,128]{1,0:T(8,128)S(1)}, u32[]{:S(2)}, u32[]{:S(2)}) %collective-permute-start.2) | collective-permute-done | bytes 327712 | tf_op jit(solution)/shard_map/ppermute | solution.py:196
  21.7 1.9 %collective-permute-start.15 = (f32[640,128]{1,0:T(8,128)S(1)}, f32[640,128]{1,0:T(8,128)S(1)}, u32[]{:S(2)}, u32[]{:S(2)}) collective-permute-start(f32[640,128]{1,0:T(8,128)S(1)} %get-tuple-element.62), channel_id=1, source_target_pairs={{0,8},{4,12},{8,16},{12,20},{16,24},{20,28},{24,32},{28,36},{32,40... | collective-permute-start | bytes 983048 | tf_op jit(solution)/shard_map/ppermute | solution.py:196
  23.6 7.2 %collective-permute-done.3.refs_4_ = f32[640,128]{1,0:T(8,128)S(1)} collective-permute-done((f32[640,128]{1,0:T(8,128)S(1)}, f32[640,128]{1,0:T(8,128)S(1)}, u32[]{:S(2)}, u32[]{:S(2)}) %collective-permute-start.3) | collective-permute-done | bytes 327712 | tf_op jit(solution)/shard_map/ppermute | solution.py:196
  30.8 3.3 %collective-permute-start.16 = (f32[640,128]{1,0:T(8,128)S(1)}, f32[640,128]{1,0:T(8,128)S(1)}, u32[]{:S(2)}, u32[]{:S(2)}) collective-permute-start(f32[640,128]{1,0:T(8,128)S(1)} %get-tuple-element.63), channel_id=1, source_target_pairs={{0,16},{4,20},{8,24},{12,28},{16,32},{20,36},{24,40},{28,44},{32,4... | collective-permute-start | bytes 983048 | tf_op jit(solution)/shard_map/ppermute | solution.py:196
  34.1 2.6 %collective-permute-done.4.refs_5_ = f32[640,128]{1,0:T(8,128)S(1)} collective-permute-done((f32[640,128]{1,0:T(8,128)S(1)}, f32[640,128]{1,0:T(8,128)S(1)}, u32[]{:S(2)}, u32[]{:S(2)}) %collective-permute-start.4) | collective-permute-done | bytes 327712 | tf_op jit(solution)/shard_map/ppermute | solution.py:196
  36.7 4.6 %collective-permute-start.17 = (f32[640,128]{1,0:T(8,128)S(1)}, f32[640,128]{1,0:T(8,128)S(1)}, u32[]{:S(2)}, u32[]{:S(2)}) collective-permute-start(f32[640,128]{1,0:T(8,128)S(1)} %get-tuple-element.64), channel_id=1, source_target_pairs={{0,24},{4,28},{8,32},{12,36},{16,40},{20,44},{24,48},{28,52},{32,5... | collective-permute-start | bytes 983048 | tf_op jit(solution)/shard_map/ppermute | solution.py:196
  42.1 4.6 %collective-permute-start.18 = (f32[640,128]{1,0:T(8,128)S(1)}, f32[640,128]{1,0:T(8,128)S(1)}, u32[]{:S(2)}, u32[]{:S(2)}) collective-permute-start(f32[640,128]{1,0:T(8,128)S(1)} %shard_map.75), channel_id=1, source_target_pairs={{0,32},{4,36},{8,40},{12,44},{16,48},{20,52},{24,56},{28,60},{32,0... | collective-permute-start | bytes 983048 | tf_op jit(solution)/shard_map/ppermute | solution.py:196
  46.7 3.1 %collective-permute-start.19 = (f32[640,128]{1,0:T(8,128)S(1)}, f32[640,128]{1,0:T(8,128)S(1)}, u32[]{:S(2)}, u32[]{:S(2)}) collective-permute-start(f32[640,128]{1,0:T(8,128)S(1)} %get-tuple-element.65), channel_id=1, source_target_pairs={{0,40},{4,44},{8,48},{12,52},{16,56},{20,60},{24,0},{28,4},{32,8},... | collective-permute-start | bytes 983048 | tf_op jit(solution)/shard_map/ppermute | solution.py:196
  49.8 3.9 %collective-permute-done.16.refs_2_ = f32[640,128]{1,0:T(8,128)S(1)} collective-permute-done((f32[640,128]{1,0:T(8,128)S(1)}, f32[640,128]{1,0:T(8,128)S(1)}, u32[]{:S(2)}, u32[]{:S(2)}) %collective-permute-start.16) | collective-permute-done | bytes 327712 | tf_op jit(solution)/shard_map/ppermute | solution.py:196
  54.6 30.0 %collective-permute-done.17.refs_3_ = f32[640,128]{1,0:T(8,128)S(1)} collective-permute-done((f32[640,128]{1,0:T(8,128)S(1)}, f32[640,128]{1,0:T(8,128)S(1)}, u32[]{:S(2)}, u32[]{:S(2)}) %collective-permute-start.17) | collective-permute-done | bytes 327712 | tf_op jit(solution)/shard_map/ppermute | solution.py:196
  84.6 8.4 %collective-permute-start.8 = (f32[640,128]{1,0:T(8,128)S(1)}, f32[640,128]{1,0:T(8,128)S(1)}, u32[]{:S(2)}, u32[]{:S(2)}) collective-permute-start(f32[640,128]{1,0:T(8,128)S(1)} %get-tuple-element.51), channel_id=1, source_target_pairs={{0,48},{4,52},{8,56},{12,60},{16,0},{20,4},{24,8},{28,12},{32,16},... | collective-permute-start | bytes 983048 | tf_op jit(solution)/shard_map/ppermute | solution.py:196
  93.0 4.0 %collective-permute-done.20.refs_6_ = f32[640,128]{1,0:T(8,128)S(1)} collective-permute-done((f32[640,128]{1,0:T(8,128)S(1)}, f32[640,128]{1,0:T(8,128)S(1)}, u32[]{:S(2)}, u32[]{:S(2)}) %collective-permute-start.20) | collective-permute-done | bytes 327712 | tf_op jit(solution)/shard_map/ppermute | solution.py:196
  97.0 4.1 %collective-permute-start.13 = (f32[320,128]{1,0:T(8,128)S(1)}, f32[320,128]{1,0:T(8,128)S(1)}, u32[]{:S(2)}, u32[]{:S(2)}) collective-permute-start(f32[320,128]{1,0:T(8,128)S(1)} %get-tuple-element.56), channel_id=1, source_target_pairs={{0,32},{4,36},{8,40},{12,44},{16,48},{20,52},{24,56},{28,60},{32,0... | collective-permute-start | bytes 491528 | tf_op jit(solution)/shard_map/ppermute | solution.py:196
  101.1 2.4 %collective-permute-done.21.refs_7_ = f32[640,128]{1,0:T(8,128)S(1)} collective-permute-done((f32[640,128]{1,0:T(8,128)S(1)}, f32[640,128]{1,0:T(8,128)S(1)}, u32[]{:S(2)}, u32[]{:S(2)}) %collective-permute-start.21) | collective-permute-done | bytes 327712 | tf_op jit(solution)/shard_map/ppermute | solution.py:196
  103.5 5.5 %collective-permute-start.14 = (f32[320,128]{1,0:T(8,128)S(1)}, f32[320,128]{1,0:T(8,128)S(1)}, u32[]{:S(2)}, u32[]{:S(2)}) collective-permute-start(f32[320,128]{1,0:T(8,128)S(1)} %get-tuple-element.58), channel_id=1, source_target_pairs={{0,32},{4,36},{8,40},{12,44},{16,48},{20,52},{24,56},{28,60},{32,0... | collective-permute-start | bytes 491528 | tf_op jit(solution)/shard_map/ppermute | solution.py:196
  109.2 6.3 %collective-permute-done.13.block = f32[320,128]{1,0:T(8,128)S(1)} collective-permute-done((f32[320,128]{1,0:T(8,128)S(1)}, f32[320,128]{1,0:T(8,128)S(1)}, u32[]{:S(2)}, u32[]{:S(2)}) %collective-permute-start.13) | collective-permute-done | bytes 163872 | tf_op jit(solution)/shard_map/ppermute | solution.py:196
  115.5 6.1 %collective-permute-start.10 = (f32[640,128]{1,0:T(8,128)S(1)}, f32[640,128]{1,0:T(8,128)S(1)}, u32[]{:S(2)}, u32[]{:S(2)}) collective-permute-start(f32[640,128]{1,0:T(8,128)S(1)} %get-tuple-element.53), channel_id=1, source_target_pairs={{0,56},{4,60},{8,0},{12,4},{16,8},{20,12},{24,16},{28,20},{32,24},... | collective-permute-start | bytes 983048 | tf_op jit(solution)/shard_map/ppermute | solution.py:196
  121.6 15.4 %collective-permute-start.11 = (f32[640,128]{1,0:T(8,128)S(1)}, f32[640,128]{1,0:T(8,128)S(1)}, u32[]{:S(2)}, u32[]{:S(2)}) collective-permute-start(f32[640,128]{1,0:T(8,128)S(1)} %get-tuple-element.54), channel_id=1, source_target_pairs={{0,24},{4,28},{8,32},{12,36},{16,40},{20,44},{24,48},{28,52},{32,5... | collective-permute-start | bytes 983048 | tf_op jit(solution)/shard_map/ppermute | solution.py:196
  137.3 3.0 %collective-permute-done.10.refs_4_ = f32[640,128]{1,0:T(8,128)S(1)} collective-permute-done((f32[640,128]{1,0:T(8,128)S(1)}, f32[640,128]{1,0:T(8,128)S(1)}, u32[]{:S(2)}, u32[]{:S(2)}) %collective-permute-start.10) | collective-permute-done | bytes 327712 | tf_op jit(solution)/shard_map/ppermute | solution.py:196
  140.4 12.5 %collective-permute-done.11.refs_5_ = f32[640,128]{1,0:T(8,128)S(1)} collective-permute-done((f32[640,128]{1,0:T(8,128)S(1)}, f32[640,128]{1,0:T(8,128)S(1)}, u32[]{:S(2)}, u32[]{:S(2)}) %collective-permute-start.11) | collective-permute-done | bytes 327712 | tf_op jit(solution)/shard_map/ppermute | solution.py:196
  152.8 2.8 %collective-permute-start.26 = (f32[640,128]{1,0:T(8,128)S(1)}, f32[640,128]{1,0:T(8,128)S(1)}, u32[]{:S(2)}, u32[]{:S(2)}) collective-permute-start(f32[640,128]{1,0:T(8,128)S(1)} %get-tuple-element.73), channel_id=1, source_target_pairs={{0,132},{4,128},{8,140},{12,136},{16,148},{20,144},{24,156},{28,15... | collective-permute-start | bytes 983048 | tf_op jit(solution)/shard_map/ppermute | solution.py:196
  157.4 2.1 %shard_map.71.early_ref = f32[3712,128]{1,0:T(8,128)S(1)} custom-call(s32[8,128]{1,0:T(8,128)S(1)} %get-tuple-element.39.takes_ref, f32[3584,128]{1,0:T(8,128)S(1)} %bitcast.34, f32[640,128]{1,0:T(8,128)S(1)} %get-tuple-element.49.refs_0_, f32[640,128]{1,0:T(8,128)S(1)} %collective-permute-done.7.refs_1_, f32[640,128]{1,0:T(8,128)S(1)} %collective-permute-done.8.refs_2_, ...), custom_call_target="tpu_custom_call" | custom-call | flops 500000000 | bytes 1048576 | tf_op jit(solution)/shard_map/pallas_call | solution.py:266
  159.5 1.9 %shard_map.72 = (f32[3584,128]{1,0:T(8,128)}, f32[3712,128]{1,0:T(8,128)S(1)}) custom-call(s32[8,128]{1,0:T(8,128)S(1)} %get-tuple-element.39.takes_ref, f32[3584,128]{1,0:T(8,128)S(1)} %bitcast.35, f32[3712,128]{1,0:T(8,128)S(1)} %shard_map.71.early_ref, f32[320,128]{1,0:T(8,128)S(1)} %collective-permute-done.13.block), custom_call_target="tpu_custom_call", output_to_operand_aliasing={{1}: (2, {})} | custom-call | flops 500000000 | bytes 1048576 | tf_op jit(solution)/shard_map/pallas_call | solution.py:270
  161.5 1.9 %shard_map.73 = (f32[3584,128]{1,0:T(8,128)}, f32[3712,128]{1,0:T(8,128)S(1)}) custom-call(s32[8,128]{1,0:T(8,128)S(1)} %get-tuple-element.39.takes_ref, f32[3584,128]{1,0:T(8,128)S(1)} %bitcast.36, f32[3712,128]{1,0:T(8,128)S(1)} %get-tuple-element.57.early_ref, ...), custom_call_target="tpu_custom_call", output_to_operand_aliasing={{1}: (2, {}), {0}: (4, {})} | custom-call | flops 500000000 | bytes 1048576 | tf_op jit(solution)/shard_map/pallas_call | solution.py:278
  164.9 4.9 %collective-permute-done.26.refs_5_ = f32[640,128]{1,0:T(8,128)S(1)} collective-permute-done((f32[640,128]{1,0:T(8,128)S(1)}, f32[640,128]{1,0:T(8,128)S(1)}, u32[]{:S(2)}, u32[]{:S(2)}) %collective-permute-start.26) | collective-permute-done | bytes 327712 | tf_op jit(solution)/shard_map/ppermute | solution.py:196
  169.8 7.6 %collective-permute-done.27.refs_6_ = f32[640,128]{1,0:T(8,128)S(1)} collective-permute-done((f32[640,128]{1,0:T(8,128)S(1)}, f32[640,128]{1,0:T(8,128)S(1)}, u32[]{:S(2)}, u32[]{:S(2)}) %collective-permute-start.27) | collective-permute-done | bytes 327712 | tf_op jit(solution)/shard_map/ppermute | solution.py:196
  177.4 5.1 %collective-permute-done.28.refs_7_ = f32[640,128]{1,0:T(8,128)S(1)} collective-permute-done((f32[640,128]{1,0:T(8,128)S(1)}, f32[640,128]{1,0:T(8,128)S(1)}, u32[]{:S(2)}, u32[]{:S(2)}) %collective-permute-start.28) | collective-permute-done | bytes 327712 | tf_op jit(solution)/shard_map/ppermute | solution.py:196
  182.5 3.6 %shard_map.77 = f32[3584,128]{1,0:T(8,128)} custom-call(s32[8,128]{1,0:T(8,128)S(1)} %get-tuple-element.39.takes_ref, f32[3584,128]{1,0:T(8,128)S(1)} %bitcast.39, f32[640,128]{1,0:T(8,128)S(1)} %get-tuple-element.68.refs_0_, f32[640,128]{1,0:T(8,128)S(1)} %collective-permute-done.22.refs_1_, f32[640,128]{1,0:T(8,128)S(1)} %collective-permute-done.23.refs_2_, ...), custom_call_target="tpu_custom_call" | custom-call | flops 500000000 | bytes 1048576 | tf_op jit(solution)/shard_map/pallas_call | solution.py:261
  (45 shorter events, 12.7 us)
Async XLA Ops:
  1.6 14.3 %copy-start.1 = (f32[224,2048]{1,0:T(8,128)S(1)}, f32[224,2048]{1,0:T(8,128)}, u32[]{:S(2)}) copy-start(f32[224,2048]{1,0:T(8,128)} %param.8) | copy-start | bytes 5505028
  3.8 6.1 %collective-permute-start = (f32[640,128]{1,0:T(8,128)S(1)}, f32[640,128]{1,0:T(8,128)S(1)}, u32[]{:S(2)}, u32[]{:S(2)}) collective-permute-start(f32[640,128]{1,0:T(8,128)S(1)} %get-tuple-element.42), channel_id=1, source_target_pairs={{0,4},{4,0},{8,12},{12,8},{16,20},{20,16},{24,28},{28,24},{32,36},... | collective-permute-start | bytes 983048 | tf_op jit(solution)/shard_map/ppermute | solution.py:196
  3.9 11.9 %collective-permute-start.1 = (f32[640,128]{1,0:T(8,128)S(1)}, f32[640,128]{1,0:T(8,128)S(1)}, u32[]{:S(2)}, u32[]{:S(2)}) collective-permute-start(f32[640,128]{1,0:T(8,128)S(1)} %get-tuple-element.43), channel_id=1, source_target_pairs={{0,64},{4,68},{8,72},{12,76},{16,80},{20,84},{24,88},{28,92},{32,9... | collective-permute-start | bytes 983048 | tf_op jit(solution)/shard_map/ppermute | solution.py:196
  5.5 16.2 %collective-permute-start.2 = (f32[640,128]{1,0:T(8,128)S(1)}, f32[640,128]{1,0:T(8,128)S(1)}, u32[]{:S(2)}, u32[]{:S(2)}) collective-permute-start(f32[640,128]{1,0:T(8,128)S(1)} %get-tuple-element.44), channel_id=1, source_target_pairs={{0,68},{4,64},{8,76},{12,72},{16,84},{20,80},{24,92},{28,88},{32,1... | collective-permute-start | bytes 983048 | tf_op jit(solution)/shard_map/ppermute | solution.py:196
  6.7 24.1 %collective-permute-start.3 = (f32[640,128]{1,0:T(8,128)S(1)}, f32[640,128]{1,0:T(8,128)S(1)}, u32[]{:S(2)}, u32[]{:S(2)}) collective-permute-start(f32[640,128]{1,0:T(8,128)S(1)} %get-tuple-element.45), channel_id=1, source_target_pairs={{0,128},{4,132},{8,136},{12,140},{16,144},{20,148},{24,152},{28,15... | collective-permute-start | bytes 983048 | tf_op jit(solution)/shard_map/ppermute | solution.py:196
  8.4 28.3 %collective-permute-start.4 = (f32[640,128]{1,0:T(8,128)S(1)}, f32[640,128]{1,0:T(8,128)S(1)}, u32[]{:S(2)}, u32[]{:S(2)}) collective-permute-start(f32[640,128]{1,0:T(8,128)S(1)} %get-tuple-element.46), channel_id=1, source_target_pairs={{0,132},{4,128},{8,140},{12,136},{16,148},{20,144},{24,156},{28,15... | collective-permute-start | bytes 983048 | tf_op jit(solution)/shard_map/ppermute | solution.py:196
  10.0 32.1 %collective-permute-start.5 = (f32[640,128]{1,0:T(8,128)S(1)}, f32[640,128]{1,0:T(8,128)S(1)}, u32[]{:S(2)}, u32[]{:S(2)}) collective-permute-start(f32[640,128]{1,0:T(8,128)S(1)} %get-tuple-element.47), channel_id=1, source_target_pairs={{0,192},{4,196},{8,200},{12,204},{16,208},{20,212},{24,216},{28,22... | collective-permute-start | bytes 983048 | tf_op jit(solution)/shard_map/ppermute | solution.py:196
  15.8 30.9 %collective-permute-start.6 = (f32[640,128]{1,0:T(8,128)S(1)}, f32[640,128]{1,0:T(8,128)S(1)}, u32[]{:S(2)}, u32[]{:S(2)}) collective-permute-start(f32[640,128]{1,0:T(8,128)S(1)} %get-tuple-element.48), channel_id=1, source_target_pairs={{0,196},{4,192},{8,204},{12,200},{16,212},{20,208},{24,220},{28,21... | collective-permute-start | bytes 983048 | tf_op jit(solution)/shard_map/ppermute | solution.py:196
  21.7 28.1 %collective-permute-start.15 = (f32[640,128]{1,0:T(8,128)S(1)}, f32[640,128]{1,0:T(8,128)S(1)}, u32[]{:S(2)}, u32[]{:S(2)}) collective-permute-start(f32[640,128]{1,0:T(8,128)S(1)} %get-tuple-element.62), channel_id=1, source_target_pairs={{0,8},{4,12},{8,16},{12,20},{16,24},{20,28},{24,32},{28,36},{32,40... | collective-permute-start | bytes 983048 | tf_op jit(solution)/shard_map/ppermute | solution.py:196
  30.8 22.9 %collective-permute-start.16 = (f32[640,128]{1,0:T(8,128)S(1)}, f32[640,128]{1,0:T(8,128)S(1)}, u32[]{:S(2)}, u32[]{:S(2)}) collective-permute-start(f32[640,128]{1,0:T(8,128)S(1)} %get-tuple-element.63), channel_id=1, source_target_pairs={{0,16},{4,20},{8,24},{12,28},{16,32},{20,36},{24,40},{28,44},{32,4... | collective-permute-start | bytes 983048 | tf_op jit(solution)/shard_map/ppermute | solution.py:196
  36.7 47.9 %collective-permute-start.17 = (f32[640,128]{1,0:T(8,128)S(1)}, f32[640,128]{1,0:T(8,128)S(1)}, u32[]{:S(2)}, u32[]{:S(2)}) collective-permute-start(f32[640,128]{1,0:T(8,128)S(1)} %get-tuple-element.64), channel_id=1, source_target_pairs={{0,24},{4,28},{8,32},{12,36},{16,40},{20,44},{24,48},{28,52},{32,5... | collective-permute-start | bytes 983048 | tf_op jit(solution)/shard_map/ppermute | solution.py:196
  42.1 42.5 %collective-permute-start.18 = (f32[640,128]{1,0:T(8,128)S(1)}, f32[640,128]{1,0:T(8,128)S(1)}, u32[]{:S(2)}, u32[]{:S(2)}) collective-permute-start(f32[640,128]{1,0:T(8,128)S(1)} %shard_map.75), channel_id=1, source_target_pairs={{0,32},{4,36},{8,40},{12,44},{16,48},{20,52},{24,56},{28,60},{32,0... | collective-permute-start | bytes 983048 | tf_op jit(solution)/shard_map/ppermute | solution.py:196
  46.7 46.3 %collective-permute-start.19 = (f32[640,128]{1,0:T(8,128)S(1)}, f32[640,128]{1,0:T(8,128)S(1)}, u32[]{:S(2)}, u32[]{:S(2)}) collective-permute-start(f32[640,128]{1,0:T(8,128)S(1)} %get-tuple-element.65), channel_id=1, source_target_pairs={{0,40},{4,44},{8,48},{12,52},{16,56},{20,60},{24,0},{28,4},{32,8},... | collective-permute-start | bytes 983048 | tf_op jit(solution)/shard_map/ppermute | solution.py:196
  49.8 47.2 %collective-permute-start.20 = (f32[640,128]{1,0:T(8,128)S(1)}, f32[640,128]{1,0:T(8,128)S(1)}, u32[]{:S(2)}, u32[]{:S(2)}) collective-permute-start(f32[640,128]{1,0:T(8,128)S(1)} %get-tuple-element.66), channel_id=1, source_target_pairs={{0,48},{4,52},{8,56},{12,60},{16,0},{20,4},{24,8},{28,12},{32,16},... | collective-permute-start | bytes 983048 | tf_op jit(solution)/shard_map/ppermute | solution.py:196
  53.7 49.8 %collective-permute-start.21 = (f32[640,128]{1,0:T(8,128)S(1)}, f32[640,128]{1,0:T(8,128)S(1)}, u32[]{:S(2)}, u32[]{:S(2)}) collective-permute-start(f32[640,128]{1,0:T(8,128)S(1)} %get-tuple-element.67), channel_id=1, source_target_pairs={{0,56},{4,60},{8,0},{12,4},{16,8},{20,12},{24,16},{28,20},{32,24},... | collective-permute-start | bytes 983048 | tf_op jit(solution)/shard_map/ppermute | solution.py:196
  54.6 102.8 %copy-start = (f32[224,2048]{1,0:T(8,128)S(1)}, f32[224,2048]{1,0:T(8,128)}, u32[]{:S(2)}) copy-start(f32[224,2048]{1,0:T(8,128)} %param.5) | copy-start | bytes 5505028
  84.6 52.5 %collective-permute-start.7 = (f32[640,128]{1,0:T(8,128)S(1)}, f32[640,128]{1,0:T(8,128)S(1)}, u32[]{:S(2)}, u32[]{:S(2)}) collective-permute-start(f32[640,128]{1,0:T(8,128)S(1)} %get-tuple-element.50), channel_id=1, source_target_pairs={{0,16},{4,20},{8,24},{12,28},{16,32},{20,36},{24,40},{28,44},{32,4... | collective-permute-start | bytes 983048 | tf_op jit(solution)/shard_map/ppermute | solution.py:196
  84.6 52.5 %collective-permute-start.8 = (f32[640,128]{1,0:T(8,128)S(1)}, f32[640,128]{1,0:T(8,128)S(1)}, u32[]{:S(2)}, u32[]{:S(2)}) collective-permute-start(f32[640,128]{1,0:T(8,128)S(1)} %get-tuple-element.51), channel_id=1, source_target_pairs={{0,48},{4,52},{8,56},{12,60},{16,0},{20,4},{24,8},{28,12},{32,16},... | collective-permute-start | bytes 983048 | tf_op jit(solution)/shard_map/ppermute | solution.py:196
  93.0 44.2 %collective-permute-start.9 = (f32[640,128]{1,0:T(8,128)S(1)}, f32[640,128]{1,0:T(8,128)S(1)}, u32[]{:S(2)}, u32[]{:S(2)}) collective-permute-start(f32[640,128]{1,0:T(8,128)S(1)} %get-tuple-element.52), channel_id=1, source_target_pairs={{0,8},{4,12},{8,16},{12,20},{16,24},{20,28},{24,32},{28,36},{32,40... | collective-permute-start | bytes 983048 | tf_op jit(solution)/shard_map/ppermute | solution.py:196
  97.0 18.5 %collective-permute-start.13 = (f32[320,128]{1,0:T(8,128)S(1)}, f32[320,128]{1,0:T(8,128)S(1)}, u32[]{:S(2)}, u32[]{:S(2)}) collective-permute-start(f32[320,128]{1,0:T(8,128)S(1)} %get-tuple-element.56), channel_id=1, source_target_pairs={{0,32},{4,36},{8,40},{12,44},{16,48},{20,52},{24,56},{28,60},{32,0... | collective-permute-start | bytes 491528 | tf_op jit(solution)/shard_map/ppermute | solution.py:196
  103.5 18.1 %collective-permute-start.14 = (f32[320,128]{1,0:T(8,128)S(1)}, f32[320,128]{1,0:T(8,128)S(1)}, u32[]{:S(2)}, u32[]{:S(2)}) collective-permute-start(f32[320,128]{1,0:T(8,128)S(1)} %get-tuple-element.58), channel_id=1, source_target_pairs={{0,32},{4,36},{8,40},{12,44},{16,48},{20,52},{24,56},{28,60},{32,0... | collective-permute-start | bytes 491528 | tf_op jit(solution)/shard_map/ppermute | solution.py:196
  115.5 24.8 %collective-permute-start.10 = (f32[640,128]{1,0:T(8,128)S(1)}, f32[640,128]{1,0:T(8,128)S(1)}, u32[]{:S(2)}, u32[]{:S(2)}) collective-permute-start(f32[640,128]{1,0:T(8,128)S(1)} %get-tuple-element.53), channel_id=1, source_target_pairs={{0,56},{4,60},{8,0},{12,4},{16,8},{20,12},{24,16},{28,20},{32,24},... | collective-permute-start | bytes 983048 | tf_op jit(solution)/shard_map/ppermute | solution.py:196
  121.6 31.2 %collective-permute-start.11 = (f32[640,128]{1,0:T(8,128)S(1)}, f32[640,128]{1,0:T(8,128)S(1)}, u32[]{:S(2)}, u32[]{:S(2)}) collective-permute-start(f32[640,128]{1,0:T(8,128)S(1)} %get-tuple-element.54), channel_id=1, source_target_pairs={{0,24},{4,28},{8,32},{12,36},{16,40},{20,44},{24,48},{28,52},{32,5... | collective-permute-start | bytes 983048 | tf_op jit(solution)/shard_map/ppermute | solution.py:196
  137.1 15.7 %collective-permute-start.12 = (f32[640,128]{1,0:T(8,128)S(1)}, f32[640,128]{1,0:T(8,128)S(1)}, u32[]{:S(2)}, u32[]{:S(2)}) collective-permute-start(f32[640,128]{1,0:T(8,128)S(1)} %get-tuple-element.55), channel_id=1, source_target_pairs={{0,40},{4,44},{8,48},{12,52},{16,56},{20,60},{24,0},{28,4},{32,8},... | collective-permute-start | bytes 983048 | tf_op jit(solution)/shard_map/ppermute | solution.py:196
  137.1 18.5 %collective-permute-start.22 = (f32[640,128]{1,0:T(8,128)S(1)}, f32[640,128]{1,0:T(8,128)S(1)}, u32[]{:S(2)}, u32[]{:S(2)}) collective-permute-start(f32[640,128]{1,0:T(8,128)S(1)} %get-tuple-element.69), channel_id=1, source_target_pairs={{0,4},{4,0},{8,12},{12,8},{16,20},{20,16},{24,28},{28,24},{32,36},... | collective-permute-start | bytes 983048 | tf_op jit(solution)/shard_map/ppermute | solution.py:196
  137.2 19.5 %collective-permute-start.23 = (f32[640,128]{1,0:T(8,128)S(1)}, f32[640,128]{1,0:T(8,128)S(1)}, u32[]{:S(2)}, u32[]{:S(2)}) collective-permute-start(f32[640,128]{1,0:T(8,128)S(1)} %get-tuple-element.70), channel_id=1, source_target_pairs={{0,64},{4,68},{8,72},{12,76},{16,80},{20,84},{24,88},{28,92},{32,9... | collective-permute-start | bytes 983048 | tf_op jit(solution)/shard_map/ppermute | solution.py:196
  140.3 23.1 %collective-permute-start.24 = (f32[640,128]{1,0:T(8,128)S(1)}, f32[640,128]{1,0:T(8,128)S(1)}, u32[]{:S(2)}, u32[]{:S(2)}) collective-permute-start(f32[640,128]{1,0:T(8,128)S(1)} %get-tuple-element.71), channel_id=1, source_target_pairs={{0,68},{4,64},{8,76},{12,72},{16,84},{20,80},{24,92},{28,88},{32,1... | collective-permute-start | bytes 983048 | tf_op jit(solution)/shard_map/ppermute | solution.py:196
  152.8 12.1 %collective-permute-start.25 = (f32[640,128]{1,0:T(8,128)S(1)}, f32[640,128]{1,0:T(8,128)S(1)}, u32[]{:S(2)}, u32[]{:S(2)}) collective-permute-start(f32[640,128]{1,0:T(8,128)S(1)} %get-tuple-element.72), channel_id=1, source_target_pairs={{0,128},{4,132},{8,136},{12,140},{16,144},{20,148},{24,152},{28,15... | collective-permute-start | bytes 983048 | tf_op jit(solution)/shard_map/ppermute | solution.py:196
  152.8 17.0 %collective-permute-start.26 = (f32[640,128]{1,0:T(8,128)S(1)}, f32[640,128]{1,0:T(8,128)S(1)}, u32[]{:S(2)}, u32[]{:S(2)}) collective-permute-start(f32[640,128]{1,0:T(8,128)S(1)} %get-tuple-element.73), channel_id=1, source_target_pairs={{0,132},{4,128},{8,140},{12,136},{16,148},{20,144},{24,156},{28,15... | collective-permute-start | bytes 983048 | tf_op jit(solution)/shard_map/ppermute | solution.py:196
  155.6 21.8 %collective-permute-start.27 = (f32[640,128]{1,0:T(8,128)S(1)}, f32[640,128]{1,0:T(8,128)S(1)}, u32[]{:S(2)}, u32[]{:S(2)}) collective-permute-start(f32[640,128]{1,0:T(8,128)S(1)} %get-tuple-element.74), channel_id=1, source_target_pairs={{0,192},{4,196},{8,200},{12,204},{16,208},{20,212},{24,216},{28,22... | collective-permute-start | bytes 983048 | tf_op jit(solution)/shard_map/ppermute | solution.py:196
  156.8 25.7 %collective-permute-start.28 = (f32[640,128]{1,0:T(8,128)S(1)}, f32[640,128]{1,0:T(8,128)S(1)}, u32[]{:S(2)}, u32[]{:S(2)}) collective-permute-start(f32[640,128]{1,0:T(8,128)S(1)} %get-tuple-element.75), channel_id=1, source_target_pairs={{0,196},{4,192},{8,204},{12,200},{16,212},{20,208},{24,220},{28,21... | collective-permute-start | bytes 983048 | tf_op jit(solution)/shard_map/ppermute | solution.py:196
  161.5 21.0 %copy-start.2 = (f32[224,2048]{1,0:T(8,128)S(1)}, f32[224,2048]{1,0:T(8,128)}, u32[]{:S(2)}) copy-start(f32[224,2048]{1,0:T(8,128)} %param.6) | copy-start | bytes 5505028
  (1 other events, 1.8 us)

commit v4 on v2

--- a/solution.py
+++ b/solution.py
@@ -83,7 +83,7 @@
 
 
 def cell(at, r):
-    return slice(at * CELL + r * TALL, at * CELL + r * TALL + TALL)
+    return pl.ds(pl.multiple_of(at * CELL + r * TALL, TALL), TALL)
 
 
 def pack(sends_ref, rows_ref, block, units):
@@ -93,6 +93,16 @@
 
 
 def pack_by_z_kernel(shifts, sends_ref, rows_ref, *blocks):
+    if len(blocks) == 1:
+
+        def fill(line, carry):
+            unit = unit_at(line, shifts[0], 1)
+            for r in range(LIMIT):
+                blocks[0][cell(line, r), :] = rows_ref[row_at(sends_ref[r, unit]), :]
+            return carry
+
+        lax.fori_loop(0, LINES, fill, 0)
+        return
     for dz, block in zip(shifts, blocks):
         pack(sends_ref, rows_ref, block, [unit_at(line, dz, 1) for line in range(LINES)])
 
@@ -142,10 +152,18 @@
         merge(takes_ref, own_ref, block, merged, [unit_at(line, dz, -1) for line in range(LINES)])
 
 
-def unpack_late_kernel(shifts, takes_ref, own_ref, early_ref, *refs):
-    blocks, (out_ref, merged, sem) = refs[: len(shifts)], refs[len(shifts) :]
-    for dz, block in zip(shifts, blocks):
-        merge(takes_ref, own_ref, block, merged, [unit_at(line, dz, -1) for line in range(LINES)])
+def unpack_late_kernel(shifts, takes_ref, own_ref, early_ref, block, *refs):
+    out_ref, merged, sem = refs
+
+    def place(line, carry):
+        unit = unit_at(line, shifts[0], -1)
+        for r in range(LIMIT):
+            start = takes_ref[r, unit]
+            own = own_ref[row_at(jnp.where(start < FLAT, start, 0)), :]
+            merged[row_at(start), :] = (own + block[cell(line, r), :]) * 0.5
+        return carry
+
+    lax.fori_loop(0, LINES, place, 0)
     store(merged, out_ref, sem)
 
 

time: 185 us -> 185 us (level)
  transfers between devices with their start and end apart: 28 -> 28, of which waited for: 14 -> 14; matrix products, arithmetic and copies ran while one was open for 0% -> 0% of each run, Pallas kernels for 3% -> 4%
where the time goes in v4:
time: 185 us
  waiting for transfers between devices  95.6 us (52%)
  starting transfers between devices  74.8 us (40%)
  Pallas kernels  12.4 us (7%)
    ppermute x28, waiting for transfers between devices, sent(): return lax.ppermute(block, UNITS, pairs)  95.6 us
    ppermute x28, starting transfers between devices, sent(): return lax.ppermute(block, UNITS, pairs)  74.8 us
  transfers between devices with their start and end apart: 28, of which 14 were waited for; matrix products, arithmetic and copies ran while one was open for 0% of the time, Pallas kernels for 4%

profile of v4, /device:TPU:199, one launch (start us, length us, event | category | flops | bytes accessed | tf_op | source)
XLA Modules:
  0.0 184.8 jit_solution(2636646853135905764)
XLA Ops:
  2.5 1.3 shard_map.69
  4.8 1.5 collective-permute-start.2
  6.2 1.8 collective-permute-start.3
  8.1 1.4 collective-permute-start.4
  9.5 1.2 shard_map.73
  11.1 2.6 %collective-permute-done.1.refs_2_ = f32[640,128]{1,0:T(8,128)S(1)} collective-permute-done((f32[640,128]{1,0:T(8,128)S(1)}, f32[640,128]{1,0:T(8,128)S(1)}, u32[]{:S(2)}, u32[]{:S(2)}) %collective-permute-start.1) | collective-permute-done | bytes 327712 | tf_op jit(solution)/shard_map/ppermute | solution.py:185
  13.8 1.9 %collective-permute-start.6 = (f32[640,128]{1,0:T(8,128)S(1)}, f32[640,128]{1,0:T(8,128)S(1)}, u32[]{:S(2)}, u32[]{:S(2)}) collective-permute-start(f32[640,128]{1,0:T(8,128)S(1)} %get-tuple-element.45), channel_id=1, source_target_pairs={{0,196},{4,192},{8,204},{12,200},{16,212},{20,208},{24,220},{28,21... | collective-permute-start | bytes 983048 | tf_op jit(solution)/shard_map/ppermute | solution.py:185
  15.7 6.2 %collective-permute-done.2.refs_3_ = f32[640,128]{1,0:T(8,128)S(1)} collective-permute-done((f32[640,128]{1,0:T(8,128)S(1)}, f32[640,128]{1,0:T(8,128)S(1)}, u32[]{:S(2)}, u32[]{:S(2)}) %collective-permute-start.2) | collective-permute-done | bytes 327712 | tf_op jit(solution)/shard_map/ppermute | solution.py:185
  22.6 2.2 %collective-permute-done.4.refs_5_ = f32[640,128]{1,0:T(8,128)S(1)} collective-permute-done((f32[640,128]{1,0:T(8,128)S(1)}, f32[640,128]{1,0:T(8,128)S(1)}, u32[]{:S(2)}, u32[]{:S(2)}) %collective-permute-start.4) | collective-permute-done | bytes 327712 | tf_op jit(solution)/shard_map/ppermute | solution.py:185
  24.8 1.8 collective-permute-start.16
  27.5 4.0 %collective-permute-done.5.refs_6_ = f32[640,128]{1,0:T(8,128)S(1)} collective-permute-done((f32[640,128]{1,0:T(8,128)S(1)}, f32[640,128]{1,0:T(8,128)S(1)}, u32[]{:S(2)}, u32[]{:S(2)}) %collective-permute-start.5) | collective-permute-done | bytes 327712 | tf_op jit(solution)/shard_map/ppermute | solution.py:185
  31.7 6.8 %collective-permute-done.6.refs_7_ = f32[640,128]{1,0:T(8,128)S(1)} collective-permute-done((f32[640,128]{1,0:T(8,128)S(1)}, f32[640,128]{1,0:T(8,128)S(1)}, u32[]{:S(2)}, u32[]{:S(2)}) %collective-permute-start.6) | collective-permute-done | bytes 327712 | tf_op jit(solution)/shard_map/ppermute | solution.py:185
  39.7 5.2 %collective-permute-done.15.refs_2_ = f32[640,128]{1,0:T(8,128)S(1)} collective-permute-done((f32[640,128]{1,0:T(8,128)S(1)}, f32[640,128]{1,0:T(8,128)S(1)}, u32[]{:S(2)}, u32[]{:S(2)}) %collective-permute-start.15) | collective-permute-done | bytes 327712 | tf_op jit(solution)/shard_map/ppermute | solution.py:185
  44.9 4.7 %collective-permute-start.20 = (f32[640,128]{1,0:T(8,128)S(1)}, f32[640,128]{1,0:T(8,128)S(1)}, u32[]{:S(2)}, u32[]{:S(2)}) collective-permute-start(f32[640,128]{1,0:T(8,128)S(1)} %get-tuple-element.61), channel_id=1, source_target_pairs={{0,56},{4,60},{8,0},{12,4},{16,8},{20,12},{24,16},{28,20},{32,24},... | collective-permute-start | bytes 983048 | tf_op jit(solution)/shard_map/ppermute | solution.py:185
  49.8 32.4 %collective-permute-done.16.refs_3_ = f32[640,128]{1,0:T(8,128)S(1)} collective-permute-done((f32[640,128]{1,0:T(8,128)S(1)}, f32[640,128]{1,0:T(8,128)S(1)}, u32[]{:S(2)}, u32[]{:S(2)}) %collective-permute-start.16) | collective-permute-done | bytes 327712 | tf_op jit(solution)/shard_map/ppermute | solution.py:185
  82.2 3.7 %collective-permute-start.8 = (f32[640,128]{1,0:T(8,128)S(1)}, f32[640,128]{1,0:T(8,128)S(1)}, u32[]{:S(2)}, u32[]{:S(2)}) collective-permute-start(f32[640,128]{1,0:T(8,128)S(1)} %get-tuple-element.48), channel_id=1, source_target_pairs={{0,48},{4,52},{8,56},{12,60},{16,0},{20,4},{24,8},{28,12},{32,16},... | collective-permute-start | bytes 983048 | tf_op jit(solution)/shard_map/ppermute | solution.py:185
  85.9 1.5 collective-permute-start.10
  87.4 2.2 %collective-permute-done.20.refs_7_ = f32[640,128]{1,0:T(8,128)S(1)} collective-permute-done((f32[640,128]{1,0:T(8,128)S(1)}, f32[640,128]{1,0:T(8,128)S(1)}, u32[]{:S(2)}, u32[]{:S(2)}) %collective-permute-start.20) | collective-permute-done | bytes 327712 | tf_op jit(solution)/shard_map/ppermute | solution.py:185
  89.6 6.0 %collective-permute-start.11 = (f32[640,128]{1,0:T(8,128)S(1)}, f32[640,128]{1,0:T(8,128)S(1)}, u32[]{:S(2)}, u32[]{:S(2)}) collective-permute-start(f32[640,128]{1,0:T(8,128)S(1)} %get-tuple-element.51), channel_id=1, source_target_pairs={{0,24},{4,28},{8,32},{12,36},{16,40},{20,44},{24,48},{28,52},{32,5... | collective-permute-start | bytes 983048 | tf_op jit(solution)/shard_map/ppermute | solution.py:185
  95.8 1.6 collective-permute-done.7.refs_1_
  97.3 8.6 %collective-permute-done.8.refs_2_ = f32[640,128]{1,0:T(8,128)S(1)} collective-permute-done((f32[640,128]{1,0:T(8,128)S(1)}, f32[640,128]{1,0:T(8,128)S(1)}, u32[]{:S(2)}, u32[]{:S(2)}) %collective-permute-start.8) | collective-permute-done | bytes 327712 | tf_op jit(solution)/shard_map/ppermute | solution.py:185
  105.9 1.1 collective-permute-start.13
  107.9 2.7 %collective-permute-done.10.refs_4_ = f32[640,128]{1,0:T(8,128)S(1)} collective-permute-done((f32[640,128]{1,0:T(8,128)S(1)}, f32[640,128]{1,0:T(8,128)S(1)}, u32[]{:S(2)}, u32[]{:S(2)}) %collective-permute-start.10) | collective-permute-done | bytes 327712 | tf_op jit(solution)/shard_map/ppermute | solution.py:185
  110.6 18.4 %collective-permute-start.22 = (f32[640,128]{1,0:T(8,128)S(1)}, f32[640,128]{1,0:T(8,128)S(1)}, u32[]{:S(2)}, u32[]{:S(2)}) collective-permute-start(f32[640,128]{1,0:T(8,128)S(1)} %get-tuple-element.64), channel_id=1, source_target_pairs={{0,64},{4,68},{8,72},{12,76},{16,80},{20,84},{24,88},{28,92},{32,9... | collective-permute-start | bytes 983048 | tf_op jit(solution)/shard_map/ppermute | solution.py:185
  129.0 23.4 %collective-permute-start.23 = (f32[640,128]{1,0:T(8,128)S(1)}, f32[640,128]{1,0:T(8,128)S(1)}, u32[]{:S(2)}, u32[]{:S(2)}) collective-permute-start(f32[640,128]{1,0:T(8,128)S(1)} %get-tuple-element.65), channel_id=1, source_target_pairs={{0,68},{4,64},{8,76},{12,72},{16,84},{20,80},{24,92},{28,88},{32,1... | collective-permute-start | bytes 983048 | tf_op jit(solution)/shard_map/ppermute | solution.py:185
  153.0 2.6 %collective-permute-start.27 = (f32[640,128]{1,0:T(8,128)S(1)}, f32[640,128]{1,0:T(8,128)S(1)}, u32[]{:S(2)}, u32[]{:S(2)}) collective-permute-start(f32[640,128]{1,0:T(8,128)S(1)} %get-tuple-element.69), channel_id=1, source_target_pairs={{0,196},{4,192},{8,204},{12,200},{16,212},{20,208},{24,220},{28,21... | collective-permute-start | bytes 983048 | tf_op jit(solution)/shard_map/ppermute | solution.py:185
  155.7 2.1 %shard_map.71.early_ref = f32[3712,128]{1,0:T(8,128)S(1)} custom-call(s32[8,128]{1,0:T(8,128)S(1)} %get-tuple-element.36.takes_ref, f32[3584,128]{1,0:T(8,128)S(1)} %bitcast.34, f32[640,128]{1,0:T(8,128)S(1)} %get-tuple-element.46.refs_0_, f32[640,128]{1,0:T(8,128)S(1)} %collective-permute-done.7.refs_1_, f32[640,128]{1,0:T(8,128)S(1)} %collective-permute-done.8.refs_2_, ...), custom_call_target="tpu_custom_call" | custom-call | flops 500000000 | bytes 1048576 | tf_op jit(solution)/shard_map/pallas_call | solution.py:253
  157.8 2.2 %shard_map.72 = (f32[3584,128]{1,0:T(8,128)}, f32[3712,128]{1,0:T(8,128)S(1)}) custom-call(s32[8,128]{1,0:T(8,128)S(1)} %get-tuple-element.36.takes_ref, f32[3584,128]{1,0:T(8,128)S(1)} %bitcast.35, f32[3712,128]{1,0:T(8,128)S(1)} %shard_map.71.early_ref, f32[640,128]{1,0:T(8,128)S(1)} %collective-permute-done.13.block), custom_call_target="tpu_custom_call", output_to_operand_aliasing={{1}: (2, {})} | custom-call | flops 500000000 | bytes 1048576 | tf_op jit(solution)/shard_map/pallas_call | solution.py:259
  159.9 7.0 %collective-permute-done.23.refs_3_ = f32[640,128]{1,0:T(8,128)S(1)} collective-permute-done((f32[640,128]{1,0:T(8,128)S(1)}, f32[640,128]{1,0:T(8,128)S(1)}, u32[]{:S(2)}, u32[]{:S(2)}) %collective-permute-start.23) | collective-permute-done | bytes 327712 | tf_op jit(solution)/shard_map/ppermute | solution.py:185
  166.9 7.1 %collective-permute-done.26.refs_6_ = f32[640,128]{1,0:T(8,128)S(1)} collective-permute-done((f32[640,128]{1,0:T(8,128)S(1)}, f32[640,128]{1,0:T(8,128)S(1)}, u32[]{:S(2)}, u32[]{:S(2)}) %collective-permute-start.26) | collective-permute-done | bytes 327712 | tf_op jit(solution)/shard_map/ppermute | solution.py:185
  174.0 7.0 %collective-permute-done.27.refs_7_ = f32[640,128]{1,0:T(8,128)S(1)} collective-permute-done((f32[640,128]{1,0:T(8,128)S(1)}, f32[640,128]{1,0:T(8,128)S(1)}, u32[]{:S(2)}, u32[]{:S(2)}) %collective-permute-start.27) | collective-permute-done | bytes 327712 | tf_op jit(solution)/shard_map/ppermute | solution.py:185
  181.0 3.5 %shard_map.76 = f32[3584,128]{1,0:T(8,128)} custom-call(s32[8,128]{1,0:T(8,128)S(1)} %get-tuple-element.36.takes_ref, f32[3584,128]{1,0:T(8,128)S(1)} %bitcast.38, f32[640,128]{1,0:T(8,128)S(1)} %get-tuple-element.62.refs_0_, f32[640,128]{1,0:T(8,128)S(1)} %collective-permute-done.21.refs_1_, f32[640,128]{1,0:T(8,128)S(1)} %collective-permute-done.22.refs_2_, ...), custom_call_target="tpu_custom_call" | custom-call | flops 500000000 | bytes 1048576 | tf_op jit(solution)/shard_map/pallas_call | solution.py:247
  (42 shorter events, 8.1 us)
Async XLA Ops:
  0.6 1.8 copy-start.3
  1.6 7.9 %copy-start.1 = (f32[224,2048]{1,0:T(8,128)S(1)}, f32[224,2048]{1,0:T(8,128)}, u32[]{:S(2)}) copy-start(f32[224,2048]{1,0:T(8,128)} %param.8) | copy-start | bytes 5505028
  3.8 6.9 %collective-permute-start = (f32[640,128]{1,0:T(8,128)S(1)}, f32[640,128]{1,0:T(8,128)S(1)}, u32[]{:S(2)}, u32[]{:S(2)}) collective-permute-start(f32[640,128]{1,0:T(8,128)S(1)} %get-tuple-element.39), channel_id=1, source_target_pairs={{0,4},{4,0},{8,12},{12,8},{16,20},{20,16},{24,28},{28,24},{32,36},... | collective-permute-start | bytes 983048 | tf_op jit(solution)/shard_map/ppermute | solution.py:185
  4.6 9.2 %collective-permute-start.1 = (f32[640,128]{1,0:T(8,128)S(1)}, f32[640,128]{1,0:T(8,128)S(1)}, u32[]{:S(2)}, u32[]{:S(2)}) collective-permute-start(f32[640,128]{1,0:T(8,128)S(1)} %get-tuple-element.40), channel_id=1, source_target_pairs={{0,64},{4,68},{8,72},{12,76},{16,80},{20,84},{24,88},{28,92},{32,9... | collective-permute-start | bytes 983048 | tf_op jit(solution)/shard_map/ppermute | solution.py:185
  4.8 17.1 %collective-permute-start.2 = (f32[640,128]{1,0:T(8,128)S(1)}, f32[640,128]{1,0:T(8,128)S(1)}, u32[]{:S(2)}, u32[]{:S(2)}) collective-permute-start(f32[640,128]{1,0:T(8,128)S(1)} %get-tuple-element.41), channel_id=1, source_target_pairs={{0,68},{4,64},{8,76},{12,72},{16,84},{20,80},{24,92},{28,88},{32,1... | collective-permute-start | bytes 983048 | tf_op jit(solution)/shard_map/ppermute | solution.py:185
  6.2 16.4 %collective-permute-start.3 = (f32[640,128]{1,0:T(8,128)S(1)}, f32[640,128]{1,0:T(8,128)S(1)}, u32[]{:S(2)}, u32[]{:S(2)}) collective-permute-start(f32[640,128]{1,0:T(8,128)S(1)} %get-tuple-element.42), channel_id=1, source_target_pairs={{0,128},{4,132},{8,136},{12,140},{16,144},{20,148},{24,152},{28,15... | collective-permute-start | bytes 983048 | tf_op jit(solution)/shard_map/ppermute | solution.py:185
  8.1 16.8 %collective-permute-start.4 = (f32[640,128]{1,0:T(8,128)S(1)}, f32[640,128]{1,0:T(8,128)S(1)}, u32[]{:S(2)}, u32[]{:S(2)}) collective-permute-start(f32[640,128]{1,0:T(8,128)S(1)} %get-tuple-element.43), channel_id=1, source_target_pairs={{0,132},{4,128},{8,140},{12,136},{16,148},{20,144},{24,156},{28,15... | collective-permute-start | bytes 983048 | tf_op jit(solution)/shard_map/ppermute | solution.py:185
  10.8 20.7 %collective-permute-start.5 = (f32[640,128]{1,0:T(8,128)S(1)}, f32[640,128]{1,0:T(8,128)S(1)}, u32[]{:S(2)}, u32[]{:S(2)}) collective-permute-start(f32[640,128]{1,0:T(8,128)S(1)} %get-tuple-element.44), channel_id=1, source_target_pairs={{0,192},{4,196},{8,200},{12,204},{16,208},{20,212},{24,216},{28,22... | collective-permute-start | bytes 983048 | tf_op jit(solution)/shard_map/ppermute | solution.py:185
  13.8 24.7 %collective-permute-start.6 = (f32[640,128]{1,0:T(8,128)S(1)}, f32[640,128]{1,0:T(8,128)S(1)}, u32[]{:S(2)}, u32[]{:S(2)}) collective-permute-start(f32[640,128]{1,0:T(8,128)S(1)} %get-tuple-element.45), channel_id=1, source_target_pairs={{0,196},{4,192},{8,204},{12,200},{16,212},{20,208},{24,220},{28,21... | collective-permute-start | bytes 983048 | tf_op jit(solution)/shard_map/ppermute | solution.py:185
  21.9 17.3 %collective-permute-start.14 = (f32[640,128]{1,0:T(8,128)S(1)}, f32[640,128]{1,0:T(8,128)S(1)}, u32[]{:S(2)}, u32[]{:S(2)}) collective-permute-start(f32[640,128]{1,0:T(8,128)S(1)} %get-tuple-element.56), channel_id=1, source_target_pairs={{0,8},{4,12},{8,16},{12,20},{16,24},{20,28},{24,32},{28,36},{32,40... | collective-permute-start | bytes 983048 | tf_op jit(solution)/shard_map/ppermute | solution.py:185
  22.6 22.3 %collective-permute-start.15 = (f32[640,128]{1,0:T(8,128)S(1)}, f32[640,128]{1,0:T(8,128)S(1)}, u32[]{:S(2)}, u32[]{:S(2)}) collective-permute-start(f32[640,128]{1,0:T(8,128)S(1)} %get-tuple-element.57), channel_id=1, source_target_pairs={{0,16},{4,20},{8,24},{12,28},{16,32},{20,36},{24,40},{28,44},{32,4... | collective-permute-start | bytes 983048 | tf_op jit(solution)/shard_map/ppermute | solution.py:185
  24.8 57.4 %collective-permute-start.16 = (f32[640,128]{1,0:T(8,128)S(1)}, f32[640,128]{1,0:T(8,128)S(1)}, u32[]{:S(2)}, u32[]{:S(2)}) collective-permute-start(f32[640,128]{1,0:T(8,128)S(1)} %get-tuple-element.58), channel_id=1, source_target_pairs={{0,24},{4,28},{8,32},{12,36},{16,40},{20,44},{24,48},{28,52},{32,5... | collective-permute-start | bytes 983048 | tf_op jit(solution)/shard_map/ppermute | solution.py:185
  31.5 50.7 %collective-permute-start.17 = (f32[640,128]{1,0:T(8,128)S(1)}, f32[640,128]{1,0:T(8,128)S(1)}, u32[]{:S(2)}, u32[]{:S(2)}) collective-permute-start(f32[640,128]{1,0:T(8,128)S(1)} %shard_map.74), channel_id=1, source_target_pairs={{0,32},{4,36},{8,40},{12,44},{16,48},{20,52},{24,56},{28,60},{32,0... | collective-permute-start | bytes 983048 | tf_op jit(solution)/shard_map/ppermute | solution.py:185
  38.5 47.4 %collective-permute-start.18 = (f32[640,128]{1,0:T(8,128)S(1)}, f32[640,128]{1,0:T(8,128)S(1)}, u32[]{:S(2)}, u32[]{:S(2)}) collective-permute-start(f32[640,128]{1,0:T(8,128)S(1)} %get-tuple-element.59), channel_id=1, source_target_pairs={{0,40},{4,44},{8,48},{12,52},{16,56},{20,60},{24,0},{28,4},{32,8},... | collective-permute-start | bytes 983048 | tf_op jit(solution)/shard_map/ppermute | solution.py:185
  39.2 46.7 %collective-permute-start.19 = (f32[640,128]{1,0:T(8,128)S(1)}, f32[640,128]{1,0:T(8,128)S(1)}, u32[]{:S(2)}, u32[]{:S(2)}) collective-permute-start(f32[640,128]{1,0:T(8,128)S(1)} %get-tuple-element.60), channel_id=1, source_target_pairs={{0,48},{4,52},{8,56},{12,60},{16,0},{20,4},{24,8},{28,12},{32,16},... | collective-permute-start | bytes 983048 | tf_op jit(solution)/shard_map/ppermute | solution.py:185
  44.9 44.6 %collective-permute-start.20 = (f32[640,128]{1,0:T(8,128)S(1)}, f32[640,128]{1,0:T(8,128)S(1)}, u32[]{:S(2)}, u32[]{:S(2)}) collective-permute-start(f32[640,128]{1,0:T(8,128)S(1)} %get-tuple-element.61), channel_id=1, source_target_pairs={{0,56},{4,60},{8,0},{12,4},{16,8},{20,12},{24,16},{28,20},{32,24},... | collective-permute-start | bytes 983048 | tf_op jit(solution)/shard_map/ppermute | solution.py:185
  49.8 105.9 %copy-start = (f32[224,2048]{1,0:T(8,128)S(1)}, f32[224,2048]{1,0:T(8,128)}, u32[]{:S(2)}) copy-start(f32[224,2048]{1,0:T(8,128)} %param.5) | copy-start | bytes 5505028
  82.2 15.1 %collective-permute-start.7 = (f32[640,128]{1,0:T(8,128)S(1)}, f32[640,128]{1,0:T(8,128)S(1)}, u32[]{:S(2)}, u32[]{:S(2)}) collective-permute-start(f32[640,128]{1,0:T(8,128)S(1)} %get-tuple-element.47), channel_id=1, source_target_pairs={{0,16},{4,20},{8,24},{12,28},{16,32},{20,36},{24,40},{28,44},{32,4... | collective-permute-start | bytes 983048 | tf_op jit(solution)/shard_map/ppermute | solution.py:185
  82.2 23.7 %collective-permute-start.8 = (f32[640,128]{1,0:T(8,128)S(1)}, f32[640,128]{1,0:T(8,128)S(1)}, u32[]{:S(2)}, u32[]{:S(2)}) collective-permute-start(f32[640,128]{1,0:T(8,128)S(1)} %get-tuple-element.48), channel_id=1, source_target_pairs={{0,48},{4,52},{8,56},{12,60},{16,0},{20,4},{24,8},{28,12},{32,16},... | collective-permute-start | bytes 983048 | tf_op jit(solution)/shard_map/ppermute | solution.py:185
  85.9 21.1 %collective-permute-start.9 = (f32[640,128]{1,0:T(8,128)S(1)}, f32[640,128]{1,0:T(8,128)S(1)}, u32[]{:S(2)}, u32[]{:S(2)}) collective-permute-start(f32[640,128]{1,0:T(8,128)S(1)} %get-tuple-element.49), channel_id=1, source_target_pairs={{0,8},{4,12},{8,16},{12,20},{16,24},{20,28},{24,32},{28,36},{32,40... | collective-permute-start | bytes 983048 | tf_op jit(solution)/shard_map/ppermute | solution.py:185
  85.9 24.7 %collective-permute-start.10 = (f32[640,128]{1,0:T(8,128)S(1)}, f32[640,128]{1,0:T(8,128)S(1)}, u32[]{:S(2)}, u32[]{:S(2)}) collective-permute-start(f32[640,128]{1,0:T(8,128)S(1)} %get-tuple-element.50), channel_id=1, source_target_pairs={{0,56},{4,60},{8,0},{12,4},{16,8},{20,12},{24,16},{28,20},{32,24},... | collective-permute-start | bytes 983048 | tf_op jit(solution)/shard_map/ppermute | solution.py:185
  89.6 39.4 %collective-permute-start.11 = (f32[640,128]{1,0:T(8,128)S(1)}, f32[640,128]{1,0:T(8,128)S(1)}, u32[]{:S(2)}, u32[]{:S(2)}) collective-permute-start(f32[640,128]{1,0:T(8,128)S(1)} %get-tuple-element.51), channel_id=1, source_target_pairs={{0,24},{4,28},{8,32},{12,36},{16,40},{20,44},{24,48},{28,52},{32,5... | collective-permute-start | bytes 983048 | tf_op jit(solution)/shard_map/ppermute | solution.py:185
  97.3 55.0 %collective-permute-start.12 = (f32[640,128]{1,0:T(8,128)S(1)}, f32[640,128]{1,0:T(8,128)S(1)}, u32[]{:S(2)}, u32[]{:S(2)}) collective-permute-start(f32[640,128]{1,0:T(8,128)S(1)} %get-tuple-element.52), channel_id=1, source_target_pairs={{0,40},{4,44},{8,48},{12,52},{16,56},{20,60},{24,0},{28,4},{32,8},... | collective-permute-start | bytes 983048 | tf_op jit(solution)/shard_map/ppermute | solution.py:185
  105.9 46.4 %collective-permute-start.13 = (f32[640,128]{1,0:T(8,128)S(1)}, f32[640,128]{1,0:T(8,128)S(1)}, u32[]{:S(2)}, u32[]{:S(2)}) collective-permute-start(f32[640,128]{1,0:T(8,128)S(1)} %get-tuple-element.53), channel_id=1, source_target_pairs={{0,32},{4,36},{8,40},{12,44},{16,48},{20,52},{24,56},{28,60},{32,0... | collective-permute-start | bytes 983048 | tf_op jit(solution)/shard_map/ppermute | solution.py:185
  107.0 45.4 %collective-permute-start.21 = (f32[640,128]{1,0:T(8,128)S(1)}, f32[640,128]{1,0:T(8,128)S(1)}, u32[]{:S(2)}, u32[]{:S(2)}) collective-permute-start(f32[640,128]{1,0:T(8,128)S(1)} %get-tuple-element.63), channel_id=1, source_target_pairs={{0,4},{4,0},{8,12},{12,8},{16,20},{20,16},{24,28},{28,24},{32,36},... | collective-permute-start | bytes 983048 | tf_op jit(solution)/shard_map/ppermute | solution.py:185
  110.6 42.4 %collective-permute-start.22 = (f32[640,128]{1,0:T(8,128)S(1)}, f32[640,128]{1,0:T(8,128)S(1)}, u32[]{:S(2)}, u32[]{:S(2)}) collective-permute-start(f32[640,128]{1,0:T(8,128)S(1)} %get-tuple-element.64), channel_id=1, source_target_pairs={{0,64},{4,68},{8,72},{12,76},{16,80},{20,84},{24,88},{28,92},{32,9... | collective-permute-start | bytes 983048 | tf_op jit(solution)/shard_map/ppermute | solution.py:185
  129.0 37.9 %collective-permute-start.23 = (f32[640,128]{1,0:T(8,128)S(1)}, f32[640,128]{1,0:T(8,128)S(1)}, u32[]{:S(2)}, u32[]{:S(2)}) collective-permute-start(f32[640,128]{1,0:T(8,128)S(1)} %get-tuple-element.65), channel_id=1, source_target_pairs={{0,68},{4,64},{8,76},{12,72},{16,84},{20,80},{24,92},{28,88},{32,1... | collective-permute-start | bytes 983048 | tf_op jit(solution)/shard_map/ppermute | solution.py:185
  152.3 14.6 %collective-permute-start.24 = (f32[640,128]{1,0:T(8,128)S(1)}, f32[640,128]{1,0:T(8,128)S(1)}, u32[]{:S(2)}, u32[]{:S(2)}) collective-permute-start(f32[640,128]{1,0:T(8,128)S(1)} %get-tuple-element.66), channel_id=1, source_target_pairs={{0,128},{4,132},{8,136},{12,140},{16,144},{20,148},{24,152},{28,15... | collective-permute-start | bytes 983048 | tf_op jit(solution)/shard_map/ppermute | solution.py:185
  152.4 14.5 %collective-permute-start.25 = (f32[640,128]{1,0:T(8,128)S(1)}, f32[640,128]{1,0:T(8,128)S(1)}, u32[]{:S(2)}, u32[]{:S(2)}) collective-permute-start(f32[640,128]{1,0:T(8,128)S(1)} %get-tuple-element.67), channel_id=1, source_target_pairs={{0,132},{4,128},{8,140},{12,136},{16,148},{20,144},{24,156},{28,15... | collective-permute-start | bytes 983048 | tf_op jit(solution)/shard_map/ppermute | solution.py:185
  152.5 21.6 %collective-permute-start.26 = (f32[640,128]{1,0:T(8,128)S(1)}, f32[640,128]{1,0:T(8,128)S(1)}, u32[]{:S(2)}, u32[]{:S(2)}) collective-permute-start(f32[640,128]{1,0:T(8,128)S(1)} %get-tuple-element.68), channel_id=1, source_target_pairs={{0,192},{4,196},{8,200},{12,204},{16,208},{20,212},{24,216},{28,22... | collective-permute-start | bytes 983048 | tf_op jit(solution)/shard_map/ppermute | solution.py:185
  153.0 28.0 %collective-permute-start.27 = (f32[640,128]{1,0:T(8,128)S(1)}, f32[640,128]{1,0:T(8,128)S(1)}, u32[]{:S(2)}, u32[]{:S(2)}) collective-permute-start(f32[640,128]{1,0:T(8,128)S(1)} %get-tuple-element.69), channel_id=1, source_target_pairs={{0,196},{4,192},{8,204},{12,200},{16,212},{20,208},{24,220},{28,21... | collective-permute-start | bytes 983048 | tf_op jit(solution)/shard_map/ppermute | solution.py:185
  157.7 23.3 %copy-start.2 = (f32[224,2048]{1,0:T(8,128)S(1)}, f32[224,2048]{1,0:T(8,128)}, u32[]{:S(2)}) copy-start(f32[224,2048]{1,0:T(8,128)} %param.6) | copy-start | bytes 5505028
